TPU v7x, 32 devices: a whole 2x2x4 slice. The times are simulated.
32 devices in a mesh: dp: 8 (over y, x, core), group: 4 (over z).
Axes of the slice: x: 2, y: 2, z: 4, core: 2. Of those that a mesh axis runs over, the one named last changes fastest.
Arguments:
- tokens: bfloat16 [10240, 768], P(('dp', 'group')), may hold values from -6 to 6
- cotangent: bfloat16 [10240, 768], P(('dp', 'group')), may hold values from -18 to 18
- patch_mask: int32 [10240], P(('dp', 'group')), may hold values 0 or 1
- image_tiles: int32 [32, 3], replicated, may hold values from 0 to 9, as said below
- patches: int32 [32, 3], replicated, may hold values from 0 to 288, as said below
- w_in: bfloat16 [288, 384], replicated, may hold values from -0.375 to 0.375
- b_in: float32 [384], replicated, may hold values from -1 to 1
- w_out: bfloat16 [384, 288], replicated, may hold values from -0.3125 to 0.3125
- ln_gain: float32 [768], replicated, may hold values from 0.5 to 1.5
- ln_shift: float32 [768], replicated, may hold values from -0.5 to 0.5
Outputs:
- dtokens: bfloat16 [10240, 768], P(('dp', 'group'))
- grad_w_in: bfloat16 [288, 384], replicated
- grad_b_in: bfloat16 [384], replicated
- grad_w_out: bfloat16 [384, 288], replicated
- grad_b_out: bfloat16 [288], replicated
- grad_gain: bfloat16 [768], replicated
- grad_shift: bfloat16 [768], replicated
Inputs may be any that keep to these rules, and one draw needn't show every extreme that they name: `image_tiles`: entry s of row d is the number of tiles of the s-th image slot of device row d, 0 for an empty slot. A device's tiles sum to at most 10, reached on some device. . An image has at most 9 tiles, reached in every draw. For an image of k tiles, patches lies between max(32, 32 * (k - 1) + 1) and 32 * k; it is 0 for an empty slot.
All inputs are finite; a program needn't handle non-finite values. No bound on the sum of `patch_mask` on one device may be relied on, other than what follows from the above.
Results may differ from a plain program's by a relative error of at most 0.0085.
Values may be sent and summed in bfloat16 or wider, within the bound.
No kernel may reach another device: no remote copies, remote signals or barrier semaphores. Data moves between devices by JAX's collectives and lax.ppermute only.
A program may use at most 64 MiB of HBM per device.

v0:
```python
import math

import jax
import jax.numpy as jnp
from jax import lax
from jax.sharding import PartitionSpec as P

PMAX = 288
TILE = 32


highest = lax.Precision.HIGHEST
ln_epsilon = 1e-05
clip_share = 0.5


def gelu_pair(preact):
    normal_cdf = 0.5 * (1.0 + lax.erf(preact * 0.7071067811865476))
    density = jnp.exp(-0.5 * preact * preact) * 0.3989422804014327
    return (preact * normal_cdf, normal_cdf + preact * density)


def tile_layout(tile_rows, tile_total):
    starts = jnp.cumsum(tile_rows, axis=1) - tile_rows
    places = jnp.arange(tile_total, dtype=jnp.int32)
    inside = (places[None, :, None] >= starts[:, None, :]) & (
        places[None, :, None] < (starts + tile_rows)[:, None, :]
    )
    offset = places[None, :, None] - starts[:, None, :]
    return (inside, offset)


def tile_tables(inside, offset, spans):
    img_hot = inside.astype(jnp.float32)
    tile_alive = jnp.sum(inside.astype(jnp.int32), axis=1)
    span_index = jnp.sum(jnp.where(inside, offset, 0), axis=1)
    span_hot = (
        (span_index[:, None] == jnp.arange(spans, dtype=jnp.int32)[None, :])
        & (tile_alive[:, None] > 0)
    ).astype(jnp.float32)
    image_index = jnp.sum(
        jnp.where(inside, jnp.arange(inside.shape[1], dtype=jnp.int32)[None, :], 0), axis=1
    )
    return (img_hot, span_hot, image_index)


def image_core(normed, dout, inside_tiles, span_hot, w_in, b_in, w_out):
    tile_total, slots = inside_tiles.shape
    spans = span_hot.shape[1]
    hidden = w_in.shape[1]
    tile_len = w_in.shape[0] // spans
    rows, width = normed.shape
    span_bf = span_hot.astype(jnp.bfloat16)
    rows_in = jnp.dot(
        span_bf, w_in.reshape(spans, tile_len * hidden), preferred_element_type=jnp.float32
    )
    rows_in = rows_in.astype(jnp.bfloat16).reshape(rows, hidden)
    cols_out = jnp.einsum(
        "tj,hjp->tph",
        span_bf,
        w_out.reshape(hidden, spans, tile_len),
        preferred_element_type=jnp.float32,
    )
    cols_out = cols_out.astype(jnp.bfloat16).reshape(rows, hidden)
    row_hot = (
        jnp.broadcast_to(inside_tiles[:, None, :], (tile_total, tile_len, slots))
        .reshape(rows, slots)
        .astype(jnp.bfloat16)
    )
    in_wide = (rows_in[:, None, :] * row_hot[:, :, None]).reshape(rows, slots * hidden)
    out_wide = (cols_out[:, None, :] * row_hot[:, :, None]).reshape(rows, slots * hidden)
    preact = (
        jnp.einsum("rc,rk->ck", normed, in_wide, preferred_element_type=jnp.float32).reshape(
            width, slots, hidden
        )
        + b_in
    )
    dz_all = jnp.einsum("rc,rk->ck", dout, out_wide, preferred_element_type=jnp.float32).reshape(
        width, slots, hidden
    )
    act, slope = gelu_pair(preact)
    act_b = act.astype(jnp.bfloat16).reshape(width, slots * hidden)
    dpre = dz_all * slope
    dpre_b = dpre.astype(jnp.bfloat16).reshape(width, slots * hidden)
    grad_b_in = jnp.sum(dpre, axis=(0, 1))
    row_mask = row_hot.astype(jnp.float32)[:, :, None]
    grad_rows_in = jnp.sum(
        jnp.einsum("rc,ck->rk", normed, dpre_b, preferred_element_type=jnp.float32).reshape(
            rows, slots, hidden
        )
        * row_mask,
        axis=1,
    )
    grad_rows_out = jnp.sum(
        jnp.einsum("rc,ck->rk", dout, act_b, preferred_element_type=jnp.float32).reshape(
            rows, slots, hidden
        )
        * row_mask,
        axis=1,
    )
    grad_w_in = jnp.einsum(
        "tj,tph->jph",
        span_hot,
        grad_rows_in.reshape(tile_total, tile_len, hidden),
        precision=highest,
    ).reshape(spans * tile_len, hidden)
    grad_w_out = jnp.einsum(
        "tj,tph->hjp",
        span_hot,
        grad_rows_out.reshape(tile_total, tile_len, hidden),
        precision=highest,
    ).reshape(hidden, spans * tile_len)
    out_sums = jnp.sum(dout.astype(jnp.float32), axis=1).reshape(tile_total, tile_len)
    grad_b_out = jnp.einsum("tj,tp->jp", span_hot, out_sums, precision=highest).reshape(-1)
    dnormed = jnp.einsum("rk,ck->rc", in_wide, dpre_b, preferred_element_type=jnp.float32).astype(
        jnp.bfloat16
    )
    return ((grad_w_in, grad_b_in, grad_w_out, grad_b_out), dnormed)


def clip_factor(total, entry_count):
    return jnp.minimum(1.0, clip_share * math.sqrt(entry_count) / jnp.sqrt(total + 1e-06))


def local(
    tokens, cotangent, patch_mask, image_tiles, patches, w_in, b_in, w_out, ln_gain, ln_shift
):
    tile_len = TILE
    spans = PMAX // TILE
    tile_total = tokens.shape[0] // tile_len
    me_index = lax.axis_index(("dp", "group"))
    own_tiles = lax.dynamic_slice_in_dim(image_tiles, me_index, 1, 0)
    own_patches = lax.dynamic_slice_in_dim(patches, me_index, 1, 0)
    inside, offset = tile_layout(own_tiles, tile_total)
    row_place = offset[..., None] * tile_len + jnp.arange(tile_len, dtype=jnp.int32)
    alive = jnp.sum(
        (inside[..., None] & (row_place < own_patches[:, None, :, None])).astype(jnp.int32), axis=2
    ).reshape(-1)
    alive_rows = (alive * patch_mask).astype(jnp.float32)
    values = tokens.astype(jnp.float32)
    center = values - jnp.mean(values, axis=1, keepdims=True)
    inv_std = lax.rsqrt(jnp.mean(center * center, axis=1, keepdims=True) + ln_epsilon)
    normal_x = center * inv_std
    normed = ((normal_x * ln_gain + ln_shift) * alive_rows[:, None]).astype(jnp.bfloat16)
    dout = (cotangent.astype(jnp.float32) * alive_rows[:, None]).astype(jnp.bfloat16)
    img_hot, span_hot, image_index = tile_tables(inside[0], offset[0], spans)
    terms, dnormed = image_core(normed, dout, inside[0], span_hot, w_in, b_in, w_out)
    d_rows = dnormed.astype(jnp.float32) * alive_rows[:, None]
    grad_gain = jnp.sum(d_rows * normal_x, axis=0)
    grad_shift = jnp.sum(d_rows, axis=0)
    scaled = d_rows * ln_gain
    inner = jnp.mean(scaled * normal_x, axis=1, keepdims=True)
    d_norm = (scaled - jnp.mean(scaled, axis=1, keepdims=True) - normal_x * inner) * inv_std
    dtokens = (cotangent.astype(jnp.float32) + d_norm).astype(jnp.bfloat16)
    grad_w_in, grad_b_in, grad_w_out, grad_b_out = terms
    pieces = (grad_w_in, grad_b_in, grad_w_out, grad_b_out, grad_gain, grad_shift)
    entry_count = sum((piece.size for piece in pieces))
    summed = lax.psum(
        (grad_w_in, grad_b_in, grad_w_out, grad_b_out, grad_gain, grad_shift), ("dp", "group")
    )
    total = sum((jnp.sum(piece * piece) for piece in summed))
    factor = clip_factor(total, entry_count)
    results = [(piece * factor).astype(jnp.bfloat16) for piece in summed]
    return (dtokens, results[0], results[1], results[2], results[3], results[4], results[5])


def solution(mesh):
    return jax.shard_map(
        local,
        mesh=mesh,
        in_specs=(
            P(("dp", "group"), None),
            P(("dp", "group"), None),
            P(("dp", "group")),
            P(),
            P(),
            P(),
            P(),
            P(),
            P(),
            P(),
        ),
        out_specs=(P(("dp", "group"), None), P(), P(), P(), P(), P(), P()),
        check_vma=False,
    )
```

profile of v0, /device:TPU:0, one launch (start us, length us, event | category | flops | bytes accessed | tf_op | source)
XLA Modules:
  0.0 177.4 jit_solution(6340706111094330395)
XLA Ops:
  7.2 0.0 copy-start
  7.2 0.0 copy-start.1
  7.2 0.0 copy-start.5
  7.2 0.0 copy-start.3
  7.2 0.0 copy-start.4
  7.2 0.0 all-reduce.4.cloned.1.call-start
  7.3 1.0 dynamic-slice_reduce_fusion
  8.3 0.1 subtract_reduce_fusion
  8.5 0.1 convert_reduce_fusion.2
  8.6 0.1 copy.38
  8.7 1.2 convert_reduce_fusion
  9.9 1.3 fusion.33
  11.2 0.1 copy.39
  11.3 0.1 fusion.56
  11.5 0.1 reshape.285
  11.5 0.1 broadcast_in_dim.6
  11.6 0.1 convert_element_type.108
  11.7 0.0 copy-done
  11.7 0.3 fusion.19
  12.1 0.2 copy.43
  12.3 0.0 copy-start.2
  12.3 0.0 copy-start.6
  12.3 1.1 reshape.284
  13.4 0.3 convolution_convert_fusion
  13.7 0.2 mul.218
  13.9 0.2 copy.37
  14.1 0.0 copy-done.5
  14.2 0.0 copy-done.1
  14.2 0.0 copy-done.3
  14.2 0.0 copy-done.4
  14.2 1.3 fusion.36
  15.5 0.0 copy-done.2
  15.5 0.0 copy-done.6
  15.5 1.4 multiply_reduce_fusion
  16.9 2.9 %fusion.80 = (f32[384]{0:T(512)S(1)}, bf16[768,3,384]{0,2,1:T(8,128)(2,1)S(1)}) fusion(f32[768,3,384]{0,2,1:T(8,128)S(1)} %fusion.36, f32[384]{0:T(512)S(1)} %copy-done.6, bf16[320,384]{0,1:T(8,128)(2,1)S(1)} %copy.43, bf16[320,3]{0,1:T(4,128)(2,1)S(1)} %convert_element_type.108, f32[320]{0:T(512)S(1)} %multiply_convert_fusion.7, ...), kind=kOutput, calls=%fused_computation.111 | convolution fusion | flops 579059328 | bytes 6051968 | tf_op jit(solution)/shard_map/rc,rk->ck/dot_general | solution.py:78
  19.8 0.0 copy-start.7
  19.8 0.8 convolution_bitcast_fusion.1
  20.7 0.9 copy.51
  21.6 0.9 multiply_reduce_fusion.1
  22.5 0.0 copy-done.7
  22.5 0.0 copy-start.8
  22.5 0.7 fusion.42
  23.3 0.9 copy.49
  24.2 0.0 all-reduce.4.cloned.1.call-update
  24.2 0.0 copy-done.8
  24.2 1.2 fusion.32
  25.5 1.3 convert_reduce_fusion.1
  26.8 0.1 reshape.293
  26.9 0.1 fusion.58
  27.0 0.1 reshape.294
  27.1 42.4 %all-reduce = (f32[384]{0:T(512)S(1)}, f32[288]{0:T(512)S(1)}, f32[768]{0:T(1024)S(1)}, f32[768]{0:T(1024)S(1)}) all-reduce(f32[384]{0:T(512)S(1)} %get-tuple-element.26, f32[288]{0:T(512)S(1)} %reshape.294, f32[768]{0:T(1024)S(1)} %get-tuple-element.7, f32[768]{0:T(1024)S(1)} %get-tuple-element.10), channel_id=1, replica_groups=mesh['dp'=8,'group'=4] {'dp','group'}, use_global_device_ids=true, to_apply=%region_12.13 | all-reduce | flops 2208 | bytes 17664 | tf_op jit(solution)/shard_map/psum | solution.py:158
  69.4 0.6 multiply_reduce_fusion.7
  70.0 0.6 multiply_reduce_fusion.8
  70.6 0.6 multiply_reduce_fusion.5
  71.2 0.6 multiply_reduce_fusion.6
  71.8 85.5 %all-reduce.4.cloned.1.call-done = (f32[288,384]{1,0:T(8,128)}, f32[384,288]{0,1:T(8,128)}) async-done(((f32[288,384]{1,0:T(8,128)}, f32[384,288]{0,1:T(8,128)}), (f32[288,384]{1,0:T(8,128)}, f32[384,288]{0,1:T(8,128)})) %all-reduce.4.cloned.1.call-update) | async-done | bytes 884752 | tf_op jit(solution)/shard_map/psum | solution.py:158
  157.4 1.7 multiply_reduce_fusion.3
  159.1 1.7 multiply_reduce_fusion.4
  164.8 1.7 multiply_convert_fusion.1
  166.5 1.7 multiply_convert_fusion.2
  168.2 0.6 multiply_convert_fusion.3
  168.8 0.6 multiply_convert_fusion.4
  169.4 0.6 multiply_convert_fusion.5
  169.9 0.6 multiply_convert_fusion.6
  (10 shorter events, 0.1 us)
Async XLA Ops:
  7.2 4.5 %copy-start = (bf16[384,288]{0,1:T(8,128)(2,1)S(1)}, bf16[384,288]{0,1:T(8,128)(2,1)}, u32[]{:S(2)}) copy-start(bf16[384,288]{0,1:T(8,128)(2,1)} %param.17) | copy-start | bytes 663556
  7.2 7.0 %copy-start.1 = (bf16[320,768]{1,0:T(8,128)(2,1)S(1)}, bf16[320,768]{1,0:T(8,128)(2,1)}, u32[]{:S(2)}) copy-start(bf16[320,768]{1,0:T(8,128)(2,1)} %param.10) | copy-start | bytes 1474564
  7.2 7.0 %copy-start.5 = (s32[320]{0:T(512)S(1)}, s32[320]{0:T(512)}, u32[]{:S(2)}) copy-start(s32[320]{0:T(512)} %param.12) | copy-start | bytes 3844
  7.2 7.0 %copy-start.3 = (f32[768]{0:T(1024)S(1)}, f32[768]{0:T(1024)}, u32[]{:S(2)}) copy-start(f32[768]{0:T(1024)} %param.18) | copy-start | bytes 9220
  7.2 7.0 %copy-start.4 = (f32[768]{0:T(1024)S(1)}, f32[768]{0:T(1024)}, u32[]{:S(2)}) copy-start(f32[768]{0:T(1024)} %param.19) | copy-start | bytes 9220
  7.2 150.1 %all-reduce.4.cloned.1.call-start = ((), (), s32[]{:S(2)}) async-start(), calls=%async_computation | async-start | bytes 1769472 | tf_op jit(solution)/shard_map/psum | solution.py:158
  12.3 3.2 %copy-start.2 = (bf16[320,768]{1,0:T(8,128)(2,1)S(1)}, bf16[320,768]{1,0:T(8,128)(2,1)}, u32[]{:S(2)}) copy-start(bf16[320,768]{1,0:T(8,128)(2,1)} %param.11) | copy-start | bytes 1474564
  12.3 3.2 %copy-start.6 = (f32[384]{0:T(512)S(1)}, f32[384]{0:T(512)}, u32[]{:S(2)}) copy-start(f32[384]{0:T(512)} %param.16) | copy-start | bytes 4612
  19.8 2.7 %copy-start.7 = (bf16[768,3,384]{0,2,1:T(8,128)(2,1)}, bf16[768,3,384]{0,2,1:T(8,128)(2,1)S(1)}, u32[]{:S(2)}) copy-start(bf16[768,3,384]{0,2,1:T(8,128)(2,1)S(1)} %get-tuple-element.27) | copy-start | bytes 5308420
  22.5 1.7 copy-start.8
Sparse Core Ops, SparseCore 0:
  24.3 132.9 all-reduce.3
where the time goes:
time: 178 us; the launch traced here: 177 us
  waiting for transfers between devices  85.5 us (48%)
  blocking collectives  42.4 us (24%)
  between operations  18.2 us (10%)
  other arithmetic  15.9 us (9%)
  matrix products  10 us (6%)
  local copies, waits for them, and re-layouts  5.25 us (3%)
    psum x1, waiting for transfers between devices, local(): lax.psum((grad_w_in, grad_b_in, grad_w_out, grad_b_out, grad_gain, grad_s...  85.5 us
    psum x1, blocking collectives, local(): lax.psum((grad_w_in, grad_b_in, grad_w_out, grad_b_out, grad_gain, grad_s...  42.4 us
    reduce_sum x6, other arithmetic, local(): total = sum((jnp.sum(piece * piece) for piece in summed))  5.86 us
    convert_element_type x6, other arithmetic, local(): results = [(piece * factor).astype(jnp.bfloat16) for piece in summed]  5.75 us
  transfers between devices with their start and end apart: 1, of which 1 were waited for; matrix products, arithmetic and copies ran while one was open for 3% of the time, Pallas kernels for 0%

commit v1 on v0

--- a/solution.py
+++ b/solution.py
@@ -1,3 +1,4 @@
+import functools
 import math
 
 import jax
@@ -105,11 +106,11 @@
         precision=highest,
     ).reshape(spans * tile_len, hidden)
     grad_w_out = jnp.einsum(
-        "tj,tph->hjp",
+        "tj,tph->jph",
         span_hot,
         grad_rows_out.reshape(tile_total, tile_len, hidden),
         precision=highest,
-    ).reshape(hidden, spans * tile_len)
+    ).reshape(spans * tile_len, hidden)
     out_sums = jnp.sum(dout.astype(jnp.float32), axis=1).reshape(tile_total, tile_len)
     grad_b_out = jnp.einsum("tj,tp->jp", span_hot, out_sums, precision=highest).reshape(-1)
     dnormed = jnp.einsum("rk,ck->rc", in_wide, dpre_b, preferred_element_type=jnp.float32).astype(
@@ -122,8 +123,77 @@
     return jnp.minimum(1.0, clip_share * math.sqrt(entry_count) / jnp.sqrt(total + 1e-06))
 
 
+AXES = ("dp", "group")
+LANES = 128
+
+
+def swap(x, mask, devices):
+    return lax.ppermute(x, AXES, [(i, i ^ mask) for i in range(devices)])
+
+
+def part(x, index, count):
+    size = x.shape[0] // count
+    return lax.dynamic_slice_in_dim(x, index * size, size, 0)
+
+
+def all_sum(flat, dp, group):
+    devices = dp * group
+    if devices & (devices - 1) or dp < 8:
+        return lax.psum(flat, AXES)
+    me = lax.axis_index(AXES)
+    pair, plane = group, 2 * group
+    side = (me // pair) % 2
+    spot = (me // plane) % 4
+    half = part(flat, side, 2) + swap(
+        part(flat, 1 - side, 2).astype(jnp.bfloat16), pair, devices
+    ).astype(jnp.float32)
+    sent = [swap(part(half, spot ^ k, 4).astype(jnp.bfloat16), k * plane, devices) for k in (1, 2, 3)]
+    own = part(half, spot, 4)
+    for one in sent:
+        own = own + one.astype(jnp.float32)
+    own = own.astype(jnp.bfloat16)
+    rest = [1 << b for b in range(devices.bit_length() - 1)]
+    rest = [m for m in rest if m not in (pair, plane, 2 * plane)]
+    while rest:
+        if len(rest) > 1:
+            low, high = rest[:2]
+            rest = rest[2:]
+            others = [swap(own, m, devices).astype(jnp.float32) for m in (low, high, low + high)]
+            own = (own.astype(jnp.float32) + others[0]) + (others[1] + others[2])
+        else:
+            own = own.astype(jnp.float32) + swap(own, rest.pop(), devices).astype(jnp.float32)
+        own = own.astype(jnp.bfloat16)
+    near = [own] + [swap(own, k * plane, devices) for k in (1, 2, 3)]
+    stack = jnp.stack(near)
+    mine = jnp.concatenate(
+        [lax.dynamic_index_in_dim(stack, spot ^ j, 0, keepdims=False) for j in range(4)]
+    )
+    other = swap(mine, pair, devices)
+    return jnp.concatenate(
+        [jnp.where(side == 0, mine, other), jnp.where(side == 0, other, mine)]
+    ).astype(jnp.float32)
+
+
+def pad_to(x, size):
+    return jnp.pad(x, (0, size - x.shape[0]))
+
+
+def all_sum_pieces(pieces, dp, group):
+    flats = [piece.reshape(-1) for piece in pieces]
+    widths = [-(-flat.shape[0] // LANES) * LANES for flat in flats]
+    flat = jnp.concatenate([pad_to(flat, width) for flat, width in zip(flats, widths)])
+    unit = LANES * 16 * 8
+    flat = pad_to(flat, -(-flat.shape[0] // unit) * unit)
+    out = all_sum(flat.reshape(-1, LANES), dp, group).reshape(-1)
+    results, at = [], 0
+    for piece, width in zip(pieces, widths):
+        results.append(out[at : at + piece.size].reshape(piece.shape))
+        at += width
+    return results
+
+
 def local(
-    tokens, cotangent, patch_mask, image_tiles, patches, w_in, b_in, w_out, ln_gain, ln_shift
+    dp, group, tokens, cotangent, patch_mask, image_tiles, patches, w_in, b_in, w_out, ln_gain, ln_shift
 ):
     tile_len = TILE
     spans = PMAX // TILE
@@ -155,18 +225,16 @@
     grad_w_in, grad_b_in, grad_w_out, grad_b_out = terms
     pieces = (grad_w_in, grad_b_in, grad_w_out, grad_b_out, grad_gain, grad_shift)
     entry_count = sum((piece.size for piece in pieces))
-    summed = lax.psum(
-        (grad_w_in, grad_b_in, grad_w_out, grad_b_out, grad_gain, grad_shift), ("dp", "group")
-    )
+    summed = all_sum_pieces(pieces, dp, group)
     total = sum((jnp.sum(piece * piece) for piece in summed))
     factor = clip_factor(total, entry_count)
     results = [(piece * factor).astype(jnp.bfloat16) for piece in summed]
-    return (dtokens, results[0], results[1], results[2], results[3], results[4], results[5])
+    return (dtokens, results[0], results[1], results[2].T, results[3], results[4], results[5])
 
 
 def solution(mesh):
     return jax.shard_map(
-        local,
+        functools.partial(local, mesh.shape["dp"], mesh.shape["group"]),
         mesh=mesh,
         in_specs=(
             P(("dp", "group"), None),

time: 178 us -> 59.5 us (0.33)
  waiting for transfers between devices: 85.5 us -> 14.7 us
  blocking collectives: 42.4 us -> 0 us
  between operations: 18.2 us -> 5.02 us
  starting transfers between devices: 0.04 us -> 13.1 us
  other arithmetic: 15.9 us -> 10.8 us
    psum x1 -> x0, waiting for transfers between devices: 85.5 us -> none  [local(): lax.psum((grad_w_in, grad_b_in, grad_w_out, grad_b_out, grad_gain, grad_s...]
    psum x1 -> x0, blocking collectives: 42.4 us -> none  [local(): lax.psum((grad_w_in, grad_b_in, grad_w_out, grad_b_out, grad_gain, grad_s...]
    ppermute x0 -> x11, waiting for transfers between devices: none -> 14.7 us  [swap(): return lax.ppermute(x, AXES, [(i, i ^ mask) for i in range(devices)])]
    ppermute x0 -> x11, starting transfers between devices: none -> 13.1 us  [swap(): return lax.ppermute(x, AXES, [(i, i ^ mask) for i in range(devices)])]
    convert_element_type x6 -> x4, other arithmetic: 5.75 us -> 1.81 us  [local(): results = [(piece * factor).astype(jnp.bfloat16) for piece in summed]]
    reduce_sum x6 -> x4, other arithmetic: 5.86 us -> 2.56 us  [local(): total = sum((jnp.sum(piece * piece) for piece in summed))]
  transfers between devices with their start and end apart: 1 -> 11, of which waited for: 1 -> 10; matrix products, arithmetic and copies ran while one was open for 3% -> 0% of each run, Pallas kernels for 0% -> 0%
where the time goes in v1:
time: 59.5 us; the launch traced here: 59.1 us
  waiting for transfers between devices  14.7 us (25%)
  starting transfers between devices  13.1 us (22%)
  other arithmetic  10.8 us (18%)
  matrix products  9.93 us (17%)
  local copies, waits for them, and re-layouts  5.53 us (9%)
  between operations  5.02 us (8%)
    ppermute x11, waiting for transfers between devices, swap(): return lax.ppermute(x, AXES, [(i, i ^ mask) for i in range(devices)])  14.7 us
    ppermute x11, starting transfers between devices, swap(): return lax.ppermute(x, AXES, [(i, i ^ mask) for i in range(devices)])  13.1 us
    dot_general x1, matrix products, image_core(): jnp.einsum('rc,rk->ck', dout, out_wide, preferred_element_type=jnp.float32)  3.03 us
    reduce_sum x4, other arithmetic, local(): total = sum((jnp.sum(piece * piece) for piece in summed))  2.56 us
    reduce_sum x1, other arithmetic, image_core(): jnp.sum(dout.astype(jnp.float32), axis=1).reshape(tile_total, tile_len)  2.36 us
    convert_element_type x4, other arithmetic, local(): results = [(piece * factor).astype(jnp.bfloat16) for piece in summed]  1.81 us
    convert_element_type x2, local copies, waits for them, and re-layouts, local(): results = [(piece * factor).astype(jnp.bfloat16) for piece in summed]  1.58 us
    reduce_sum x1, other arithmetic, local(): jnp.mean(center * center, axis=1, keepdims=True) + ln_epsilon  1.31 us
  transfers between devices with their start and end apart: 11, of which 10 were waited for; matrix products, arithmetic and copies ran while one was open for 0% of the time, Pallas kernels for 0%

profile of v1, /device:TPU:0, one launch (start us, length us, event | category | flops | bytes accessed | tf_op | source)
XLA Modules:
  0.0 59.1 jit_solution(2989673026260978154)
XLA Ops:
  0.7 0.9 %constant_dynamic-slice_fusion.1 = s32[1,3]{0,1:T(4,128)S(1)} fusion(s32[32,3]{0,1:T(4,128)} %param.13, s32[]{:T(128)S(6)} %select_n.69), kind=kLoop, calls=%fused_computation.117 | loop fusion | bytes 28 | tf_op jit(solution)/shard_map/dynamic_slice | solution.py:202
  1.6 0.9 %subtract_reduce_fusion = (s32[3]{0:T(128)S(1)}, s32[3]{0:T(128)S(1)}, s32[3]{0:T(128)S(1)}) fusion(s32[1,3]{0,1:T(4,128)S(1)} %reduce_window_sum.13, s32[32,3]{0,1:T(4,128)} %param.14, s32[]{:T(128)S(6)} %select_n.69, s32[32,3]{0,1:T(4,128)} %param.13), kind=kLoop, calls=%fused_computation.134 | loop fusion | flops 3 | bytes 76 | tf_op jit(solution)/shard_map/sub | solution.py:25
  2.5 0.1 convert_reduce_fusion.2
  2.6 0.1 copy.38
  2.7 1.2 %convert_reduce_fusion = f32[320]{0:T(512)S(1)} fusion(bf16[320,768]{1,0:T(8,128)(2,1)} %param.10), kind=kLoop, calls=%fused_computation.22 | loop fusion | flops 491200 | bytes 492800 | tf_op jit(solution)/shard_map/reduce_sum | solution.py:211
  3.9 1.3 %fusion.33 = f32[320]{0:T(512)S(1)} fusion(bf16[320,768]{1,0:T(8,128)(2,1)} %param.10, f32[320]{0:T(512)S(1)} %broadcast_multiply_fusion.2), kind=kLoop, calls=%fused_computation.41 | loop fusion | flops 982720 | bytes 494080 | tf_op jit(solution)/shard_map/reduce_sum | solution.py:212
  5.3 0.1 copy.39
  5.4 0.1 fusion.59
  5.5 0.1 reshape.310
  5.6 0.1 broadcast_in_dim.6
  5.7 0.1 convert_element_type.176
  5.8 0.3 fusion.19
  6.1 0.2 copy.43
  6.4 1.1 %reshape.309 = bf16[9,12288]{1,0:T(8,128)(2,1)S(1)} reshape(bf16[288,384]{1,0:T(8,128)(2,1)} %param.15) | data formatting | bytes 442368 | tf_op jit(solution)/shard_map/reshape | solution.py:56
  7.5 0.3 convolution_convert_fusion
  7.8 0.2 mul.245
  8.0 0.2 copy.37
  8.3 1.3 %fusion.36 = f32[768,3,384]{0,2,1:T(8,128)S(1)} fusion(bf16[320,3]{0,1:T(4,128)(2,1)S(1)} %convert_element_type.176, bf16[320,384]{0,1:T(8,128)(2,1)S(1)} %copy.37, bf16[320,768]{1,0:T(8,128)(2,1)S(1)} %copy-done.1, f32[768]{0:T(1024)S(1)} %copy-done.4, f32[768]{0:T(1024)S(1)} %copy-done.3, f32[320]{0:T(512)S(1)} %add_rsqrt_fusion, ...), kind=kOutput, calls=%fused_computation.46 | convolution fusion | flops 569425920 | bytes 4288128 | tf_op jit(solution)/shard_map/rc,rk->ck/dot_general | solution.py:74
  9.6 1.3 %multiply_reduce_fusion = f32[320,384]{1,0:T(8,128)S(1)} fusion(f32[768,3,384]{0,2,1:T(8,128)S(1)} %fusion.36, f32[384]{0:T(512)S(1)} %copy-done.6, f32[320,3]{0,1:T(4,128)S(1)} %convert_element_type.188, bf16[320,768]{1,0:T(8,128)(2,1)S(1)} %copy-done.2, f32[320]{0:T(512)S(1)} %multiply_convert_fusion.6), kind=kOutput, calls=%fused_computation.14 | convolution fusion | flops 572891136 | bytes 4528640 | tf_op jit(solution)/shard_map/rc,ck->rk/dot_general | solution.py:96
  10.9 3.0 %fusion.89 = (f32[384]{0:T(512)S(1)}, bf16[768,3,384]{0,2,1:T(8,128)(2,1)S(1)}) fusion(f32[768,3,384]{0,2,1:T(8,128)S(1)} %fusion.36, f32[384]{0:T(512)S(1)} %copy-done.6, bf16[320,384]{0,1:T(8,128)(2,1)S(1)} %copy.43, bf16[320,3]{0,1:T(4,128)(2,1)S(1)} %convert_element_type.176, f32[320]{0:T(512)S(1)} %multiply_convert_fusion.6, ...), kind=kOutput, calls=%fused_computation.142 | convolution fusion | flops 579059328 | bytes 6051968 | tf_op jit(solution)/shard_map/rc,rk->ck/dot_general | solution.py:79
  13.9 0.9 %multiply_reduce_fusion.1 = f32[320,384]{1,0:T(8,128)S(1)} fusion(bf16[768,3,384]{0,2,1:T(8,128)(2,1)S(1)} %get-tuple-element.40, f32[320,3]{0,1:T(4,128)S(1)} %convert_element_type.188, bf16[320,768]{1,0:T(8,128)(2,1)S(1)} %copy-done.1, f32[768]{0:T(1024)S(1)} %copy-done.4, f32[768]{0:T(1024)S(1)} %copy-done.3, f32[320]{0:T(512)S(1)} %add_rsqrt_fusion, ...), kind=kOutput, calls=%fused_computation.15 | convolution fusion | flops 568565760 | bytes 2766336 | tf_op jit(solution)/shard_map/rc,ck->rk/dot_general | solution.py:89
  14.8 1.2 %fusion.32 = (f32[768]{0:T(1024)S(1)}, f32[320]{0:T(512)S(1)}, f32[320]{0:T(512)S(1)}, f32[768]{0:T(1024)S(1)}, f32[320,768]{1,0:T(8,128)S(1)}) fusion(bf16[320,768]{1,0:T(8,128)(2,1)S(1)} %copy-done.1, f32[320]{0:T(512)S(1)} %add_rsqrt_fusion, f32[320]{0:T(512)S(1)} %broadcast_multiply_fusion.2, f32[768]{0:T(1024)S(1)} %copy-done.3, ...), kind=kOutput, calls=%fused_computation.40 | convolution fusion | flops 569792384 | bytes 3507328 | tf_op jit(solution)/shard_map/rk,ck->rc/dot_general | solution.py:116
  16.0 0.7 %fusion.41 = f32[9,32,384]{2,0,1:T(8,128)S(1)} fusion(f32[10,32,384]{2,1,0:T(8,128)S(1)} %bitcast.96, s32[10]{0:T(128)S(1)} %get-tuple-element.18, pred[10]{0:T(512)(128)(4,1)S(1)} %broadcast_compare_fusion), kind=kOutput, calls=%fused_computation.52 | convolution fusion | flops 13271220 | bytes 933938 | tf_op jit(solution)/shard_map/tj,tph->jph/dot_general | solution.py:108
  16.8 0.1 copy.51
  17.0 2.4 %convert_reduce_fusion.1 = (f32[320]{0:T(512)S(1)}, bf16[320,768]{1,0:T(8,128)(2,1)}) fusion(f32[320]{0:T(512)S(1)} %multiply_convert_fusion.6, bf16[320,768]{1,0:T(8,128)(2,1)} %param.11, f32[320]{0:T(512)S(1)} %broadcast_multiply_fusion, f32[320]{0:T(512)S(1)} %add_rsqrt_fusion, f32[320]{0:T(512)S(1)} %broadcast_multiply_fusion.2, ...), kind=kLoop, calls=%fused_computation.44 | loop fusion | flops 3686080 | bytes 2468352 | tf_op jit(solution)/shard_map/reduce_sum | solution.py:114
  19.4 0.1 reshape.316
  19.4 0.1 fusion.61
  19.6 0.1 reshape.317
  19.6 0.8 %fusion.43 = f32[9,32,384]{2,0,1:T(8,128)S(1)} fusion(f32[10,32,384]{2,1,0:T(8,128)S(1)} %bitcast.95, s32[10]{0:T(128)S(1)} %get-tuple-element.18, pred[10]{0:T(512)(128)(4,1)S(1)} %broadcast_compare_fusion), kind=kOutput, calls=%fused_computation.54 | convolution fusion | flops 13271220 | bytes 933938 | tf_op jit(solution)/shard_map/tj,tph->jph/dot_general | solution.py:102
  20.4 0.1 copy.49
  20.6 0.1 constant_dynamic-update-slice_fusion.3
  20.8 0.1 pad_bitcast_fusion
  20.9 0.6 collective-permute-start
  21.5 1.1 %collective-permute-done = bf16[896,128]{1,0:T(8,128)(2,1)S(1)} collective-permute-done((bf16[896,128]{1,0:T(8,128)(2,1)S(1)}, bf16[896,128]{1,0:T(8,128)(2,1)S(1)}, u32[]{:S(2)}, u32[]{:S(2)}) %collective-permute-start) | collective-permute-done | bytes 229408 | tf_op jit(solution)/shard_map/ppermute | solution.py:131
  22.7 2.9 %collective-permute-start.1 = (bf16[224,128]{1,0:T(8,128)(2,1)S(1)}, bf16[224,128]{1,0:T(8,128)(2,1)S(1)}, u32[]{:S(2)}, u32[]{:S(2)}) collective-permute-start(bf16[224,128]{1,0:T(8,128)(2,1)S(1)} %get-tuple-element.30), channel_id=1, source_target_pairs={{0,8},{1,9},{2,10},{3,11},{4,12},{5,13},{6,14},{7,15},{8,0},{9,1},... | collective-permute-start | bytes 172040 | tf_op jit(solution)/shard_map/ppermute | solution.py:131
  25.6 1.5 %collective-permute-start.3 = (bf16[224,128]{1,0:T(8,128)(2,1)S(1)}, bf16[224,128]{1,0:T(8,128)(2,1)S(1)}, u32[]{:S(2)}, u32[]{:S(2)}) collective-permute-start(bf16[224,128]{1,0:T(8,128)(2,1)S(1)} %get-tuple-element.31), channel_id=1, source_target_pairs={{0,24},{1,25},{2,26},{3,27},{4,28},{5,29},{6,30},{7,31},{8,16},{9,... | collective-permute-start | bytes 172040 | tf_op jit(solution)/shard_map/ppermute | solution.py:131
  27.1 0.0 collective-permute-start.2
  27.1 0.7 %collective-permute-done.1 = bf16[224,128]{1,0:T(8,128)(2,1)S(1)} collective-permute-done((bf16[224,128]{1,0:T(8,128)(2,1)S(1)}, bf16[224,128]{1,0:T(8,128)(2,1)S(1)}, u32[]{:S(2)}, u32[]{:S(2)}) %collective-permute-start.1) | collective-permute-done | bytes 57376 | tf_op jit(solution)/shard_map/ppermute | solution.py:131
  27.8 2.9 %collective-permute-done.3 = bf16[224,128]{1,0:T(8,128)(2,1)S(1)} collective-permute-done((bf16[224,128]{1,0:T(8,128)(2,1)S(1)}, bf16[224,128]{1,0:T(8,128)(2,1)S(1)}, u32[]{:S(2)}, u32[]{:S(2)}) %collective-permute-start.3) | collective-permute-done | bytes 57376 | tf_op jit(solution)/shard_map/ppermute | solution.py:131
  30.7 0.9 %collective-permute-done.2 = bf16[224,128]{1,0:T(8,128)(2,1)S(1)} collective-permute-done((bf16[224,128]{1,0:T(8,128)(2,1)S(1)}, bf16[224,128]{1,0:T(8,128)(2,1)S(1)}, u32[]{:S(2)}, u32[]{:S(2)}) %collective-permute-start.2) | collective-permute-done | bytes 57376 | tf_op jit(solution)/shard_map/ppermute | solution.py:131
  31.6 3.7 %collective-permute-start.6 = (bf16[224,128]{1,0:T(8,128)(2,1)S(1)}, bf16[224,128]{1,0:T(8,128)(2,1)S(1)}, u32[]{:S(2)}, u32[]{:S(2)}) collective-permute-start(bf16[224,128]{1,0:T(8,128)(2,1)S(1)} %add_convert_fusion.1), channel_id=1, source_target_pairs={{0,3},{1,2},{2,1},{3,0},{4,7},{5,6},{6,5},{7,4},{8,11},{9,10},{10,... | collective-permute-start | bytes 172040 | tf_op jit(solution)/shard_map/ppermute | solution.py:131
  35.3 0.8 %collective-permute-start.4 = (bf16[224,128]{1,0:T(8,128)(2,1)S(1)}, bf16[224,128]{1,0:T(8,128)(2,1)S(1)}, u32[]{:S(2)}, u32[]{:S(2)}) collective-permute-start(bf16[224,128]{1,0:T(8,128)(2,1)S(1)} %add_convert_fusion.1), channel_id=1, source_target_pairs={{0,1},{1,0},{2,3},{3,2},{4,5},{5,4},{6,7},{7,6},{8,9},{9,8},{10,11... | collective-permute-start | bytes 172040 | tf_op jit(solution)/shard_map/ppermute | solution.py:131
  36.0 2.1 %collective-permute-done.6 = bf16[224,128]{1,0:T(8,128)(2,1)S(1)} collective-permute-done((bf16[224,128]{1,0:T(8,128)(2,1)S(1)}, bf16[224,128]{1,0:T(8,128)(2,1)S(1)}, u32[]{:S(2)}, u32[]{:S(2)}) %collective-permute-start.6) | collective-permute-done | bytes 57376 | tf_op jit(solution)/shard_map/ppermute | solution.py:131
  38.1 2.2 %collective-permute-done.5 = bf16[224,128]{1,0:T(8,128)(2,1)S(1)} collective-permute-done((bf16[224,128]{1,0:T(8,128)(2,1)S(1)}, bf16[224,128]{1,0:T(8,128)(2,1)S(1)}, u32[]{:S(2)}, u32[]{:S(2)}) %collective-permute-start.5) | collective-permute-done | bytes 57376 | tf_op jit(solution)/shard_map/ppermute | solution.py:131
  40.4 1.5 %collective-permute-start.9 = (bf16[224,128]{1,0:T(8,128)(2,1)S(1)}, bf16[224,128]{1,0:T(8,128)(2,1)S(1)}, u32[]{:S(2)}, u32[]{:S(2)}) collective-permute-start(bf16[224,128]{1,0:T(8,128)(2,1)S(1)} %add_convert_fusion), channel_id=1, source_target_pairs={{0,24},{1,25},{2,26},{3,27},{4,28},{5,29},{6,30},{7,31},{8,16},{9,... | collective-permute-start | bytes 172040 | tf_op jit(solution)/shard_map/ppermute | solution.py:131
  41.9 1.3 %collective-permute-start.8 = (bf16[224,128]{1,0:T(8,128)(2,1)S(1)}, bf16[224,128]{1,0:T(8,128)(2,1)S(1)}, u32[]{:S(2)}, u32[]{:S(2)}) collective-permute-start(bf16[224,128]{1,0:T(8,128)(2,1)S(1)} %add_convert_fusion), channel_id=1, source_target_pairs={{0,16},{1,17},{2,18},{3,19},{4,20},{5,21},{6,22},{7,23},{8,24},{9,... | collective-permute-start | bytes 172040 | tf_op jit(solution)/shard_map/ppermute | solution.py:131
  43.2 0.8 %collective-permute-start.7 = (bf16[224,128]{1,0:T(8,128)(2,1)S(1)}, bf16[224,128]{1,0:T(8,128)(2,1)S(1)}, u32[]{:S(2)}, u32[]{:S(2)}) collective-permute-start(bf16[224,128]{1,0:T(8,128)(2,1)S(1)} %add_convert_fusion), channel_id=1, source_target_pairs={{0,8},{1,9},{2,10},{3,11},{4,12},{5,13},{6,14},{7,15},{8,0},{9,1},... | collective-permute-start | bytes 172040 | tf_op jit(solution)/shard_map/ppermute | solution.py:131
  43.9 1.9 %collective-permute-done.9 = bf16[224,128]{1,0:T(8,128)(2,1)S(1)} collective-permute-done((bf16[224,128]{1,0:T(8,128)(2,1)S(1)}, bf16[224,128]{1,0:T(8,128)(2,1)S(1)}, u32[]{:S(2)}, u32[]{:S(2)}) %collective-permute-start.9) | collective-permute-done | bytes 57376 | tf_op jit(solution)/shard_map/ppermute | solution.py:131
  45.8 0.6 collective-permute-done.8
  46.4 1.0 %collective-permute-done.7 = bf16[224,128]{1,0:T(8,128)(2,1)S(1)} collective-permute-done((bf16[224,128]{1,0:T(8,128)(2,1)S(1)}, bf16[224,128]{1,0:T(8,128)(2,1)S(1)}, u32[]{:S(2)}, u32[]{:S(2)}) %collective-permute-start.7) | collective-permute-done | bytes 57376 | tf_op jit(solution)/shard_map/ppermute | solution.py:131
  47.5 0.1 collective-permute-start.10
  47.5 1.5 %collective-permute-done.10 = bf16[896,128]{1,0:T(8,128)(2,1)S(1)} collective-permute-done((bf16[896,128]{1,0:T(8,128)(2,1)S(1)}, bf16[896,128]{1,0:T(8,128)(2,1)S(1)}, u32[]{:S(2)}, u32[]{:S(2)}) %collective-permute-start.10) | collective-permute-done | bytes 229408 | tf_op jit(solution)/shard_map/ppermute | solution.py:131
  49.0 0.1 broadcast_select_fusion.1
  49.1 0.1 fusion.55
  49.2 0.6 %multiply_reduce_fusion.7 = f32[]{:T(128)} fusion(f32[1792,128]{1,0:T(8,128)S(1)} %get-tuple-element.27), kind=kLoop, calls=%fused_computation.126 | loop fusion | flops 767 | bytes 1540 | tf_op jit(solution)/shard_map/reduce_sum | solution.py:229
  49.8 0.6 %multiply_reduce_fusion.5 = (f32[]{:T(128)}, f32[]{:T(128)}) fusion(f32[1792,128]{1,0:T(8,128)S(1)} %get-tuple-element.27), kind=kLoop, calls=%fused_computation.104 | loop fusion | flops 3070 | bytes 6152 | tf_op jit(solution)/shard_map/reduce_sum | solution.py:229
  50.4 0.8 %multiply_reduce_fusion.3 = (f32[]{:T(128)}, f32[]{:T(128)}) fusion(f32[1792,128]{1,0:T(8,128)S(1)} %get-tuple-element.27), kind=kLoop, calls=%fused_computation.64 | loop fusion | flops 442366 | bytes 884744 | tf_op jit(solution)/shard_map/reduce_sum | solution.py:229
  51.2 0.6 %fusion.78 = f32[]{:T(128)} fusion(bf16[229376]{0:T(1024)(128)(2,1)S(1)} %get-tuple-element.26), kind=kLoop, calls=%fused_computation.120 | loop fusion | flops 863 | bytes 580 | tf_op jit(solution)/shard_map/reduce_sum | solution.py:229
  55.7 0.6 fusion.79
  56.3 0.6 fusion.85
  56.8 0.6 fusion.82
  57.4 0.1 multiply_convert_fusion.1
  57.5 0.8 %convert_element_type.212 = bf16[288,384]{1,0:T(8,128)(2,1)} reshape(bf16[864,128]{1,0:T(8,128)(2,1)S(1)} %get-tuple-element.22) | data formatting | bytes 442368 | tf_op jit(solution)/shard_map/convert_element_type | solution.py:231
  58.3 0.8 %convert_element_type.208 = bf16[288,384]{1,0:T(8,128)(2,1)} reshape(bf16[864,128]{1,0:T(8,128)(2,1)S(1)} %get-tuple-element.23) | data formatting | bytes 442368 | tf_op jit(solution)/shard_map/convert_element_type | solution.py:231
  (41 shorter events, 0.5 us)
Async XLA Ops:
  0.6 5.1 %copy-start = (bf16[384,288]{0,1:T(8,128)(2,1)S(1)}, bf16[384,288]{0,1:T(8,128)(2,1)}, u32[]{:S(2)}) copy-start(bf16[384,288]{0,1:T(8,128)(2,1)} %param.17) | copy-start | bytes 663556
  0.6 7.6 %copy-start.1 = (bf16[320,768]{1,0:T(8,128)(2,1)S(1)}, bf16[320,768]{1,0:T(8,128)(2,1)}, u32[]{:S(2)}) copy-start(bf16[320,768]{1,0:T(8,128)(2,1)} %param.10) | copy-start | bytes 1474564
  0.7 7.5 %copy-start.5 = (s32[320]{0:T(512)S(1)}, s32[320]{0:T(512)}, u32[]{:S(2)}) copy-start(s32[320]{0:T(512)} %param.12) | copy-start | bytes 3844
  0.7 7.6 %copy-start.3 = (f32[768]{0:T(1024)S(1)}, f32[768]{0:T(1024)}, u32[]{:S(2)}) copy-start(f32[768]{0:T(1024)} %param.18) | copy-start | bytes 9220
  0.7 7.6 %copy-start.4 = (f32[768]{0:T(1024)S(1)}, f32[768]{0:T(1024)}, u32[]{:S(2)}) copy-start(f32[768]{0:T(1024)} %param.19) | copy-start | bytes 9220
  6.4 3.2 %copy-start.2 = (bf16[320,768]{1,0:T(8,128)(2,1)S(1)}, bf16[320,768]{1,0:T(8,128)(2,1)}, u32[]{:S(2)}) copy-start(bf16[320,768]{1,0:T(8,128)(2,1)} %param.11) | copy-start | bytes 1474564
  6.4 3.2 %copy-start.6 = (f32[384]{0:T(512)S(1)}, f32[384]{0:T(512)}, u32[]{:S(2)}) copy-start(f32[384]{0:T(512)} %param.16) | copy-start | bytes 4612
  20.9 1.7 %collective-permute-start = (bf16[896,128]{1,0:T(8,128)(2,1)S(1)}, bf16[896,128]{1,0:T(8,128)(2,1)S(1)}, u32[]{:S(2)}, u32[]{:S(2)}) collective-permute-start(bf16[896,128]{1,0:T(8,128)(2,1)S(1)} %dynamic-slice_convert_fusion), channel_id=1, source_target_pairs={{0,4},{1,5},{2,6},{3,7},{4,0},{5,1},{6,2},{7,3},{8,12},{9,13},{10,... | collective-permute-start | bytes 688136 | tf_op jit(solution)/shard_map/ppermute | solution.py:131
  22.7 5.1 %collective-permute-start.1 = (bf16[224,128]{1,0:T(8,128)(2,1)S(1)}, bf16[224,128]{1,0:T(8,128)(2,1)S(1)}, u32[]{:S(2)}, u32[]{:S(2)}) collective-permute-start(bf16[224,128]{1,0:T(8,128)(2,1)S(1)} %get-tuple-element.30), channel_id=1, source_target_pairs={{0,8},{1,9},{2,10},{3,11},{4,12},{5,13},{6,14},{7,15},{8,0},{9,1},... | collective-permute-start | bytes 172040 | tf_op jit(solution)/shard_map/ppermute | solution.py:131
  25.6 5.1 %collective-permute-start.3 = (bf16[224,128]{1,0:T(8,128)(2,1)S(1)}, bf16[224,128]{1,0:T(8,128)(2,1)S(1)}, u32[]{:S(2)}, u32[]{:S(2)}) collective-permute-start(bf16[224,128]{1,0:T(8,128)(2,1)S(1)} %get-tuple-element.31), channel_id=1, source_target_pairs={{0,24},{1,25},{2,26},{3,27},{4,28},{5,29},{6,30},{7,31},{8,16},{9,... | collective-permute-start | bytes 172040 | tf_op jit(solution)/shard_map/ppermute | solution.py:131
  27.1 4.5 %collective-permute-start.2 = (bf16[224,128]{1,0:T(8,128)(2,1)S(1)}, bf16[224,128]{1,0:T(8,128)(2,1)S(1)}, u32[]{:S(2)}, u32[]{:S(2)}) collective-permute-start(bf16[224,128]{1,0:T(8,128)(2,1)S(1)} %get-tuple-element.32), channel_id=1, source_target_pairs={{0,16},{1,17},{2,18},{3,19},{4,20},{5,21},{6,22},{7,23},{8,24},{9,... | collective-permute-start | bytes 172040 | tf_op jit(solution)/shard_map/ppermute | solution.py:131
  31.6 6.5 %collective-permute-start.6 = (bf16[224,128]{1,0:T(8,128)(2,1)S(1)}, bf16[224,128]{1,0:T(8,128)(2,1)S(1)}, u32[]{:S(2)}, u32[]{:S(2)}) collective-permute-start(bf16[224,128]{1,0:T(8,128)(2,1)S(1)} %add_convert_fusion.1), channel_id=1, source_target_pairs={{0,3},{1,2},{2,1},{3,0},{4,7},{5,6},{6,5},{7,4},{8,11},{9,10},{10,... | collective-permute-start | bytes 172040 | tf_op jit(solution)/shard_map/ppermute | solution.py:131
  35.3 5.1 %collective-permute-start.5 = (bf16[224,128]{1,0:T(8,128)(2,1)S(1)}, bf16[224,128]{1,0:T(8,128)(2,1)S(1)}, u32[]{:S(2)}, u32[]{:S(2)}) collective-permute-start(bf16[224,128]{1,0:T(8,128)(2,1)S(1)} %add_convert_fusion.1), channel_id=1, source_target_pairs={{0,2},{1,3},{2,0},{3,1},{4,6},{5,7},{6,4},{7,5},{8,10},{9,11},{10,... | collective-permute-start | bytes 172040 | tf_op jit(solution)/shard_map/ppermute | solution.py:131
  35.3 5.1 %collective-permute-start.4 = (bf16[224,128]{1,0:T(8,128)(2,1)S(1)}, bf16[224,128]{1,0:T(8,128)(2,1)S(1)}, u32[]{:S(2)}, u32[]{:S(2)}) collective-permute-start(bf16[224,128]{1,0:T(8,128)(2,1)S(1)} %add_convert_fusion.1), channel_id=1, source_target_pairs={{0,1},{1,0},{2,3},{3,2},{4,5},{5,4},{6,7},{7,6},{8,9},{9,8},{10,11... | collective-permute-start | bytes 172040 | tf_op jit(solution)/shard_map/ppermute | solution.py:131
  40.4 5.4 %collective-permute-start.9 = (bf16[224,128]{1,0:T(8,128)(2,1)S(1)}, bf16[224,128]{1,0:T(8,128)(2,1)S(1)}, u32[]{:S(2)}, u32[]{:S(2)}) collective-permute-start(bf16[224,128]{1,0:T(8,128)(2,1)S(1)} %add_convert_fusion), channel_id=1, source_target_pairs={{0,24},{1,25},{2,26},{3,27},{4,28},{5,29},{6,30},{7,31},{8,16},{9,... | collective-permute-start | bytes 172040 | tf_op jit(solution)/shard_map/ppermute | solution.py:131
  41.9 4.5 %collective-permute-start.8 = (bf16[224,128]{1,0:T(8,128)(2,1)S(1)}, bf16[224,128]{1,0:T(8,128)(2,1)S(1)}, u32[]{:S(2)}, u32[]{:S(2)}) collective-permute-start(bf16[224,128]{1,0:T(8,128)(2,1)S(1)} %add_convert_fusion), channel_id=1, source_target_pairs={{0,16},{1,17},{2,18},{3,19},{4,20},{5,21},{6,22},{7,23},{8,24},{9,... | collective-permute-start | bytes 172040 | tf_op jit(solution)/shard_map/ppermute | solution.py:131
  43.2 4.2 %collective-permute-start.7 = (bf16[224,128]{1,0:T(8,128)(2,1)S(1)}, bf16[224,128]{1,0:T(8,128)(2,1)S(1)}, u32[]{:S(2)}, u32[]{:S(2)}) collective-permute-start(bf16[224,128]{1,0:T(8,128)(2,1)S(1)} %add_convert_fusion), channel_id=1, source_target_pairs={{0,8},{1,9},{2,10},{3,11},{4,12},{5,13},{6,14},{7,15},{8,0},{9,1},... | collective-permute-start | bytes 172040 | tf_op jit(solution)/shard_map/ppermute | solution.py:131
  47.5 1.6 %collective-permute-start.10 = (bf16[896,128]{1,0:T(8,128)(2,1)S(1)}, bf16[896,128]{1,0:T(8,128)(2,1)S(1)}, u32[]{:S(2)}, u32[]{:S(2)}) collective-permute-start(bf16[896,128]{1,0:T(8,128)(2,1)S(1)} %pad_maximum_fusion.2), channel_id=1, source_target_pairs={{0,4},{1,5},{2,6},{3,7},{4,0},{5,1},{6,2},{7,3},{8,12},{9,13},{10,... | collective-permute-start | bytes 688136 | tf_op jit(solution)/shard_map/ppermute | solution.py:131

commit v2 on v0

v2 whole, which is shorter than its diff:
```python
import functools
import math

import jax
import jax.numpy as jnp
from jax import lax
from jax.experimental import pallas as pl
from jax.experimental.pallas import tpu as pltpu
from jax.sharding import PartitionSpec as P

TILE = 32
LANES = 128
AXES = ("dp", "group")
ln_epsilon = 1e-05
clip_share = 0.5
f32 = jnp.float32
bf16 = jnp.bfloat16
NN = (((1,), (0,)), ((), ()))
NT = (((1,), (1,)), ((), ()))


def dot(left, right, dims=NN):
    return lax.dot_general(left, right, dims, preferred_element_type=f32)


def as_column(row):
    return jnp.transpose(jnp.broadcast_to(row, (LANES, row.shape[1])))


def lane_blocks(x):
    return [x[:, at : at + LANES] for at in range(0, x.shape[1], LANES)]


def fold_lanes(x):
    return functools.reduce(jnp.add, lane_blocks(x))


def row_total(x):
    return jnp.sum(fold_lanes(x), axis=1, keepdims=True)


def half_rows(places, hidden, width):
    used = (hidden // LANES) * places + hidden // LANES + width // LANES
    return -(-used // 64) * 64


def grad_kernel(
    pair,
    me_ref,
    tiles_ref,
    patches_ref,
    tok_ref,
    cot_ref,
    mask_ref,
    w_in_ref,
    b_in_ref,
    w_out_ref,
    gain_ref,
    shift_ref,
    dtok_ref,
    keep_ref,
    send_ref,
    flat_ref,
    y_s,
    o_s,
    dn_s,
    w_in_t,
    w_out_s,
    bias_s,
    alive_s,
    mean_s,
    inv_s,
    gin_s,
    gout_s,
    bin_s,
    bout_s,
):
    rows, width = tok_ref.shape
    places, hidden = w_in_ref.shape
    slots = tiles_ref.shape[0]
    me = me_ref[0]
    tiles = [tiles_ref[s, me] for s in range(slots)]
    counts = [patches_ref[s, me] for s in range(slots)]
    firsts = [sum(tiles[:s], jnp.int32(0)) * TILE for s in range(slots)]
    half = keep_ref.shape[0]
    side = (me // pair) % 2
    gain = gain_ref[...].reshape(1, width)
    shift = shift_ref[...].reshape(1, width)

    w_in_t[...] = jnp.transpose(w_in_ref[...])
    w_out_s[...] = jnp.transpose(w_out_ref[...])
    bias_s[...] = as_column(b_in_ref[...].reshape(1, hidden))
    gin_s[...] = jnp.zeros(gin_s.shape, f32)
    gout_s[...] = jnp.zeros(gout_s.shape, f32)
    bin_s[...] = jnp.zeros(bin_s.shape, f32)
    bout_s[...] = jnp.zeros(bout_s.shape, f32)

    mask_row = mask_ref[...].astype(f32).reshape(1, rows)
    short = -rows % LANES
    kept = as_column(jnp.concatenate([mask_row, jnp.zeros((1, short), f32)], axis=1))[:rows]
    row = lax.broadcasted_iota(jnp.int32, (rows, LANES), 0)
    inside = functools.reduce(
        jnp.logical_or,
        [(row >= first) & (row < first + count) for first, count in zip(firsts, counts)],
    )
    alive_s[...] = jnp.where(inside, kept, 0.0)

    step = 64
    for at in range(0, rows, step):
        piece = slice(at, at + step)
        values = tok_ref[piece, :].astype(f32)
        mean = row_total(values) * (1.0 / width)
        center = values - mean
        inv_std = lax.rsqrt(row_total(center * center) * (1.0 / width) + ln_epsilon)
        mean_s[piece, :] = jnp.broadcast_to(mean, (step, LANES))
        inv_s[piece, :] = jnp.broadcast_to(inv_std, (step, LANES))
        alive = alive_s[piece, :1]
        y_s[piece, :] = ((center * inv_std * gain + shift) * alive).astype(bf16)
        o_s[piece, :] = (cot_ref[piece, :].astype(f32) * alive).astype(bf16)
    tail = slice(rows, y_s.shape[0])
    y_s[tail, :] = jnp.zeros((places, width), bf16)
    o_s[tail, :] = jnp.zeros((places, width), bf16)

    chunk = 256
    third = places // 3

    def image(first, count, window):
        first = pl.multiple_of(first, TILE)
        limit = count * TILE
        lane = lax.broadcasted_iota(jnp.int32, (hidden, window), 1)
        own_in = jnp.where(lane < limit, w_in_t[:, :window].astype(f32), 0.0).astype(bf16)
        own_out = jnp.where(lane < limit, w_out_s[:, :window].astype(f32), 0.0).astype(bf16)
        bias = jnp.concatenate([bias_s[...]] * (chunk // LANES), axis=1)
        gin = jnp.zeros((window, hidden), f32)
        gout = jnp.zeros((window, hidden), f32)
        bin_sum = jnp.zeros((hidden, LANES), f32)
        bout_sum = jnp.zeros((window, LANES), f32)
        for at in range(0, width, chunk):
            cols = slice(at, at + chunk)
            y = y_s[pl.ds(first, window), cols]
            o = o_s[pl.ds(first, window), cols]
            preact = dot(own_in, y) + bias
            dz = dot(own_out, o)
            normal_cdf = 0.5 + 0.5 * lax.erf(preact * 0.7071067811865476)
            density = jnp.exp(-0.5 * preact * preact) * 0.3989422804014327
            act = (preact * normal_cdf).astype(bf16)
            dpre = dz * (normal_cdf + preact * density)
            dpre_b = dpre.astype(bf16)
            bin_sum += fold_lanes(dpre)
            bout_sum += fold_lanes(o.astype(f32))
            gin += dot(y, dpre_b, NT)
            gout += dot(o, act, NT)
            dn_s[pl.ds(first, window), cols] = dot(w_in_ref[:window, :], dpre_b).astype(bf16)
        place = lax.broadcasted_iota(jnp.int32, (window, LANES), 0)
        own = place < limit
        wide = lax.broadcasted_iota(jnp.int32, (window, hidden), 0) < limit
        gin_s[:window, :] += jnp.where(wide, gin, 0.0)
        gout_s[:window, :] += jnp.where(wide, gout, 0.0)
        bin_s[...] += bin_sum
        bout_s[:window, :] += jnp.where(own, bout_sum, 0.0)

    for first, count in zip(firsts, tiles):
        for size in (1, 2, 3):
            low, high = (size - 1) * third // TILE, size * third // TILE

            @pl.when((count > low) & (count <= high))
            def _():
                image(first, count, size * third)

    gain_sum = jnp.zeros((8, width), f32)
    shift_sum = jnp.zeros((8, width), f32)
    for at in range(0, rows, step):
        piece = slice(at, at + step)
        alive = alive_s[piece, :1]
        inv_std = inv_s[piece, :1]
        normal_x = (tok_ref[piece, :].astype(f32) - mean_s[piece, :1]) * inv_std
        d_rows = jnp.where(alive > 0.0, dn_s[piece, :].astype(f32), 0.0)
        scaled_x = d_rows * normal_x
        gain_sum += jnp.sum(scaled_x.reshape(step // 8, 8, width), axis=0)
        shift_sum += jnp.sum(d_rows.reshape(step // 8, 8, width), axis=0)
        scaled = d_rows * gain
        middle = row_total(scaled) * (1.0 / width)
        inner = row_total(scaled_x * gain) * (1.0 / width)
        d_norm = (scaled - middle - normal_x * inner) * inv_std
        dtok_ref[piece, :] = (cot_ref[piece, :].astype(f32) + d_norm).astype(bf16)

    blocks = hidden // LANES
    small = blocks * places
    pairs = (
        (gin_s, bin_s[...], gain_sum),
        (gout_s, bout_s[...], shift_sum),
    )
    for which, (weights, bias_part, wide_part) in enumerate(pairs):
        base = which * half
        for j in range(blocks):
            flat_ref[base + j * places : base + (j + 1) * places, :] = weights[
                :, j * LANES : (j + 1) * LANES
            ]
        flat_ref[base + small : base + half, :] = jnp.zeros((half - small, LANES), f32)
        bias_row = jnp.sum(jnp.transpose(bias_part), axis=0, keepdims=True)
        wide_row = jnp.sum(wide_part, axis=0, keepdims=True)
        at = base + small
        for block in lane_blocks(bias_row) + lane_blocks(wide_row):
            flat_ref[at : at + 1, :] = block
            at += 1
    keep_ref[...] = flat_ref[pl.ds(pl.multiple_of(side * half, 16), half), :]
    send_ref[...] = flat_ref[pl.ds(pl.multiple_of((1 - side) * half, 16), half), :].astype(bf16)


def all_terms(pair, me, tokens, cotangent, mask, image_tiles, patches, w_in, b_in, w_out, gain, shift):
    rows, width = tokens.shape
    places, hidden = w_in.shape
    half = half_rows(places, hidden, width)
    smem = pl.BlockSpec(memory_space=pltpu.SMEM)
    vmem = pl.BlockSpec(memory_space=pltpu.VMEM)
    return pl.pallas_call(
        functools.partial(grad_kernel, pair),
        name="terms",
        out_shape=(
            jax.ShapeDtypeStruct((rows, width), bf16),
            pltpu.VMEM((half, LANES), f32),
            pltpu.VMEM((half, LANES), bf16),
        ),
        in_specs=[smem] * 3 + [vmem] * 8,
        out_specs=(vmem, vmem, vmem),
        scratch_shapes=[
            pltpu.VMEM((2 * half, LANES), f32),
            pltpu.VMEM((rows + places, width), bf16),
            pltpu.VMEM((rows + places, width), bf16),
            pltpu.VMEM((rows + places, width), bf16),
            pltpu.VMEM((hidden, places), bf16),
            pltpu.VMEM((hidden, places), bf16),
            pltpu.VMEM((hidden, LANES), f32),
            pltpu.VMEM((rows, LANES), f32),
            pltpu.VMEM((rows, LANES), f32),
            pltpu.VMEM((rows, LANES), f32),
            pltpu.VMEM((places, hidden), f32),
            pltpu.VMEM((places, hidden), f32),
            pltpu.VMEM((hidden, LANES), f32),
            pltpu.VMEM((hidden, LANES), f32),
        ],
    )(
        me.reshape(1),
        image_tiles.T,
        patches.T,
        tokens,
        cotangent,
        mask,
        w_in,
        b_in,
        w_out.T,
        gain,
        shift,
    )


def swap(x, mask, devices):
    return lax.ppermute(x, AXES, [(i, i ^ mask) for i in range(devices)])


def part(x, index, count):
    size = x.shape[0] // count
    return lax.dynamic_slice_in_dim(x, index * size, size, 0)


def all_sum(keep, send, dp, group):
    devices = dp * group
    me = lax.axis_index(AXES)
    pair, plane = group, 2 * group
    spot = (me // plane) % 4
    if devices & (devices - 1) or dp < 8:
        raise NotImplementedError("device count")
    half = keep + swap(send, pair, devices).astype(f32)
    sent = [swap(part(half, spot ^ k, 4).astype(bf16), k * plane, devices) for k in (1, 2, 3)]
    own = part(half, spot, 4)
    for one in sent:
        own = own + one.astype(f32)
    own = own.astype(bf16)
    rest = [1 << b for b in range(devices.bit_length() - 1)]
    rest = [m for m in rest if m not in (pair, plane, 2 * plane)]
    while rest:
        if len(rest) > 1:
            low, high = rest[:2]
            rest = rest[2:]
            others = [swap(own, m, devices).astype(f32) for m in (low, high, low + high)]
            own = (own.astype(f32) + others[0]) + (others[1] + others[2])
        else:
            own = own.astype(f32) + swap(own, rest.pop(), devices).astype(f32)
        own = own.astype(bf16)
    near = [own] + [swap(own, k * plane, devices) for k in (1, 2, 3)]
    return near, swap(jnp.concatenate(near), pair, devices)


def clip_kernel(
    pair,
    me_ref,
    near0,
    near1,
    near2,
    near3,
    far_ref,
    w_in_ref,
    b_in_ref,
    w_out_ref,
    b_out_ref,
    gain_ref,
    shift_ref,
    sum_s,
):
    places, hidden = w_in_ref.shape
    width = gain_ref.shape[0]
    size = near0.shape[0]
    half = 4 * size
    me = me_ref[0]
    side = (me // pair) % 2
    spot = (me // (2 * pair)) % 4
    total = jnp.zeros((8, LANES), f32)
    for k, near in enumerate((near0, near1, near2, near3)):
        spread = (spot ^ k) * size
        mine = near[...].astype(f32)
        other = far_ref[k * size : (k + 1) * size, :].astype(f32)
        sum_s[pl.ds(pl.multiple_of(side * half + spread, 16), size), :] = mine
        sum_s[pl.ds(pl.multiple_of((1 - side) * half + spread, 16), size), :] = other
        squares = mine * mine + other * other
        total += jnp.sum(squares.reshape(size // 8, 8, LANES), axis=0)
    total = jnp.sum(total)
    entries = 2 * places * hidden + hidden + places + 2 * width
    total = jnp.full((1, LANES), total, f32)
    factor = jnp.minimum(1.0, clip_share * math.sqrt(entries) * lax.rsqrt(total + 1e-06))
    blocks = hidden // LANES
    small = blocks * places
    for j in range(blocks):
        lanes = slice(j * LANES, (j + 1) * LANES)
        at = j * places
        w_in_ref[:, lanes] = (sum_s[at : at + places, :] * factor).astype(bf16)
        w_out_ref[:, lanes] = (sum_s[half + at : half + at + places, :] * factor).astype(bf16)
    for base, bias_ref, wide_ref in ((0, b_in_ref, gain_ref), (half, b_out_ref, shift_ref)):
        at = base + small
        row = jnp.concatenate([sum_s[at + j : at + j + 1, :] for j in range(blocks)], axis=1)
        size = bias_ref.shape[0]
        bias_ref[...] = (row * factor[:, :1])[:, :size].astype(bf16).reshape(size)
        at += blocks
        row = jnp.concatenate(
            [sum_s[at + j : at + j + 1, :] for j in range(width // LANES)], axis=1
        )
        wide_ref[...] = (row * factor[:, :1]).astype(bf16).reshape(width)


def clipped(pair, me, near, far, places, hidden, width):
    smem = pl.BlockSpec(memory_space=pltpu.SMEM)
    vmem = pl.BlockSpec(memory_space=pltpu.VMEM)
    shapes = [(places, hidden), (hidden,), (places, hidden), (places,), (width,), (width,)]
    outs = pl.pallas_call(
        functools.partial(clip_kernel, pair),
        name="clip",
        out_shape=tuple(jax.ShapeDtypeStruct(shape, bf16) for shape in shapes),
        in_specs=[smem] + [vmem] * 5,
        out_specs=(vmem,) * 6,
        scratch_shapes=[pltpu.VMEM((2 * far.shape[0], LANES), f32)],
    )(me.reshape(1), *[pltpu.with_memory_space_constraint(x, pltpu.VMEM) for x in (*near, far)])
    return outs[0], outs[1], outs[2].T, *outs[3:]


def local(
    dp,
    group,
    tokens,
    cotangent,
    patch_mask,
    image_tiles,
    patches,
    w_in,
    b_in,
    w_out,
    ln_gain,
    ln_shift,
):
    me = lax.axis_index(AXES)
    dtokens, keep, send = all_terms(
        group,
        me,
        tokens,
        cotangent,
        patch_mask,
        image_tiles,
        patches,
        w_in,
        b_in,
        w_out,
        ln_gain,
        ln_shift,
    )
    near, far = all_sum(keep, send, dp, group)
    grads = clipped(group, me, near, far, *w_in.shape, tokens.shape[1])
    return (dtokens, *grads)


def solution(mesh):
    return jax.shard_map(
        functools.partial(local, mesh.shape["dp"], mesh.shape["group"]),
        mesh=mesh,
        in_specs=(
            P(AXES, None),
            P(AXES, None),
            P(AXES),
            P(),
            P(),
            P(),
            P(),
            P(),
            P(),
            P(),
        ),
        out_specs=(P(AXES, None), P(), P(), P(), P(), P(), P()),
        check_vma=False,
    )
```

time: 178 us -> 37.2 us (0.21)
  waiting for transfers between devices: 85.5 us -> 13.8 us
  blocking collectives: 42.4 us -> 0 us
  between operations: 18.2 us -> 0.68 us
  other arithmetic: 15.9 us -> 0.12 us
  starting transfers between devices: 0.04 us -> 14.1 us
  matrix products: 10 us -> 0 us
  Pallas kernels: 0 us -> 7.89 us
  local copies, waits for them, and re-layouts: 5.25 us -> 0.04 us
    psum x1 -> x0, waiting for transfers between devices: 85.5 us -> none  [local(): lax.psum((grad_w_in, grad_b_in, grad_w_out, grad_b_out, grad_gain, grad_s...]
    psum x1 -> x0, blocking collectives: 42.4 us -> none  [local(): lax.psum((grad_w_in, grad_b_in, grad_w_out, grad_b_out, grad_gain, grad_s...]
    ppermute x0 -> x11, starting transfers between devices: none -> 14.1 us  [swap(): return lax.ppermute(x, AXES, [(i, i ^ mask) for i in range(devices)])]
    ppermute x0 -> x11, waiting for transfers between devices: none -> 13.8 us  [swap(): return lax.ppermute(x, AXES, [(i, i ^ mask) for i in range(devices)])]
    dot_general x10 -> x0, matrix products: 10 us -> none  [the longest x1 2.89 us: image_core(): jnp.einsum('rc,rk->ck', dout, out_wide, preferred_element_type=jnp.float32)]
    reduce_sum x11 -> x0, other arithmetic: 9.93 us -> none  [the longest x6 5.86 us: local(): total = sum((jnp.sum(piece * piece) for piece in summed))]
    pallas_call x0 -> x2, Pallas kernels: none -> 7.89 us  [the longest x1 6.79 us: all_terms(): pl.pallas_call(functools.partial(grad_kernel, pair), name='terms', out_sh...]
    convert_element_type x9 -> x2, other arithmetic: 5.77 us -> 0.07 us  [all_sum(): own = own.astype(bf16)]
  transfers between devices with their start and end apart: 1 -> 11, of which waited for: 1 -> 11; matrix products, arithmetic and copies ran while one was open for 3% -> 0% of each run, Pallas kernels for 0% -> 0%
where the time goes in v2:
time: 37.2 us; the launch traced here: 36.7 us
  starting transfers between devices  14.1 us (38%)
  waiting for transfers between devices  13.8 us (37%)
  Pallas kernels  7.89 us (21%)
  between operations  0.68 us (2%)
    ppermute x11, starting transfers between devices, swap(): return lax.ppermute(x, AXES, [(i, i ^ mask) for i in range(devices)])  14.1 us
    ppermute x11, waiting for transfers between devices, swap(): return lax.ppermute(x, AXES, [(i, i ^ mask) for i in range(devices)])  13.8 us
    pallas_call x1, Pallas kernels, all_terms(): pl.pallas_call(functools.partial(grad_kernel, pair), name='terms', out_sh...  6.79 us
    pallas_call x1, Pallas kernels, clipped(): pl.pallas_call(functools.partial(clip_kernel, pair), name='clip', out_sha...  1.1 us
  transfers between devices with their start and end apart: 11, of which 11 were waited for; matrix products, arithmetic and copies ran while one was open for 0% of the time, Pallas kernels for 0%

profile of v2, /device:TPU:0, one launch (start us, length us, event | category | flops | bytes accessed | tf_op | source)
XLA Modules:
  0.0 36.7 jit_solution(16340669971750952084)
XLA Ops:
  0.6 6.8 %terms.1 = (bf16[320,768]{1,0:T(8,128)(2,1)}, f32[896,128]{1,0:T(8,128)S(1)}, bf16[896,128]{1,0:T(8,128)(2,1)S(1)}) custom-call(s32[1]{0:T(128)} %bitcast.me_ref, s32[3,32]{1,0:T(4,128)} %bitcast.6, s32[3,32]{1,0:T(4,128)} %bitcast.7, bf16[320,768]{1,0:T(8,128)(2,1)} %tok_ref.1, bf16[320,768]{1,0:T(8,128)(2,1)} %cot_ref.1, s32[320]{0:T(512)} %mask_ref.1, ...), custom_call_target="tpu_custom_call" | custom-call | tf_op jit(solution)/shard_map/terms/pallas_call | solution.py:216
  7.4 1.7 %collective-permute-start = (bf16[896,128]{1,0:T(8,128)(2,1)S(1)}, bf16[896,128]{1,0:T(8,128)(2,1)S(1)}, u32[]{:S(2)}, u32[]{:S(2)}) collective-permute-start(bf16[896,128]{1,0:T(8,128)(2,1)S(1)} %get-tuple-element.18), channel_id=1, source_target_pairs={{0,4},{1,5},{2,6},{3,7},{4,0},{5,1},{6,2},{7,3},{8,12},{9,13},{10,... | collective-permute-start | bytes 688136 | tf_op jit(solution)/shard_map/ppermute | solution.py:258
  9.1 1.1 %collective-permute-done = bf16[896,128]{1,0:T(8,128)(2,1)S(1)} collective-permute-done((bf16[896,128]{1,0:T(8,128)(2,1)S(1)}, bf16[896,128]{1,0:T(8,128)(2,1)S(1)}, u32[]{:S(2)}, u32[]{:S(2)}) %collective-permute-start) | collective-permute-done | bytes 229408 | tf_op jit(solution)/shard_map/ppermute | solution.py:258
  10.3 2.7 %collective-permute-start.3 = (bf16[224,128]{1,0:T(8,128)(2,1)S(1)}, bf16[224,128]{1,0:T(8,128)(2,1)S(1)}, u32[]{:S(2)}, u32[]{:S(2)}) collective-permute-start(bf16[224,128]{1,0:T(8,128)(2,1)S(1)} %get-tuple-element.26), channel_id=1, source_target_pairs={{0,24},{1,25},{2,26},{3,27},{4,28},{5,29},{6,30},{7,31},{8,16},{9,... | collective-permute-start | bytes 172040 | tf_op jit(solution)/shard_map/ppermute | solution.py:258
  13.0 0.7 %collective-permute-start.2 = (bf16[224,128]{1,0:T(8,128)(2,1)S(1)}, bf16[224,128]{1,0:T(8,128)(2,1)S(1)}, u32[]{:S(2)}, u32[]{:S(2)}) collective-permute-start(bf16[224,128]{1,0:T(8,128)(2,1)S(1)} %get-tuple-element.27), channel_id=1, source_target_pairs={{0,16},{1,17},{2,18},{3,19},{4,20},{5,21},{6,22},{7,23},{8,24},{9,... | collective-permute-start | bytes 172040 | tf_op jit(solution)/shard_map/ppermute | solution.py:258
  13.7 1.0 %collective-permute-start.1 = (bf16[224,128]{1,0:T(8,128)(2,1)S(1)}, bf16[224,128]{1,0:T(8,128)(2,1)S(1)}, u32[]{:S(2)}, u32[]{:S(2)}) collective-permute-start(bf16[224,128]{1,0:T(8,128)(2,1)S(1)} %get-tuple-element.25), channel_id=1, source_target_pairs={{0,8},{1,9},{2,10},{3,11},{4,12},{5,13},{6,14},{7,15},{8,0},{9,1},... | collective-permute-start | bytes 172040 | tf_op jit(solution)/shard_map/ppermute | solution.py:258
  14.7 0.8 %collective-permute-done.3 = bf16[224,128]{1,0:T(8,128)(2,1)S(1)} collective-permute-done((bf16[224,128]{1,0:T(8,128)(2,1)S(1)}, bf16[224,128]{1,0:T(8,128)(2,1)S(1)}, u32[]{:S(2)}, u32[]{:S(2)}) %collective-permute-start.3) | collective-permute-done | bytes 57376 | tf_op jit(solution)/shard_map/ppermute | solution.py:258
  15.4 1.7 %collective-permute-done.2 = bf16[224,128]{1,0:T(8,128)(2,1)S(1)} collective-permute-done((bf16[224,128]{1,0:T(8,128)(2,1)S(1)}, bf16[224,128]{1,0:T(8,128)(2,1)S(1)}, u32[]{:S(2)}, u32[]{:S(2)}) %collective-permute-start.2) | collective-permute-done | bytes 57376 | tf_op jit(solution)/shard_map/ppermute | solution.py:258
  17.2 0.8 %collective-permute-done.1 = bf16[224,128]{1,0:T(8,128)(2,1)S(1)} collective-permute-done((bf16[224,128]{1,0:T(8,128)(2,1)S(1)}, bf16[224,128]{1,0:T(8,128)(2,1)S(1)}, u32[]{:S(2)}, u32[]{:S(2)}) %collective-permute-start.1) | collective-permute-done | bytes 57376 | tf_op jit(solution)/shard_map/ppermute | solution.py:258
  18.0 3.1 %collective-permute-start.6 = (bf16[224,128]{1,0:T(8,128)(2,1)S(1)}, bf16[224,128]{1,0:T(8,128)(2,1)S(1)}, u32[]{:S(2)}, u32[]{:S(2)}) collective-permute-start(bf16[224,128]{1,0:T(8,128)(2,1)S(1)} %add_convert_fusion.1), channel_id=1, source_target_pairs={{0,3},{1,2},{2,1},{3,0},{4,7},{5,6},{6,5},{7,4},{8,11},{9,10},{10,... | collective-permute-start | bytes 172040 | tf_op jit(solution)/shard_map/ppermute | solution.py:258
  21.1 1.1 %collective-permute-start.5 = (bf16[224,128]{1,0:T(8,128)(2,1)S(1)}, bf16[224,128]{1,0:T(8,128)(2,1)S(1)}, u32[]{:S(2)}, u32[]{:S(2)}) collective-permute-start(bf16[224,128]{1,0:T(8,128)(2,1)S(1)} %add_convert_fusion.1), channel_id=1, source_target_pairs={{0,2},{1,3},{2,0},{3,1},{4,6},{5,7},{6,4},{7,5},{8,10},{9,11},{10,... | collective-permute-start | bytes 172040 | tf_op jit(solution)/shard_map/ppermute | solution.py:258
  22.2 0.3 collective-permute-start.4
  22.4 1.8 %collective-permute-done.6 = bf16[224,128]{1,0:T(8,128)(2,1)S(1)} collective-permute-done((bf16[224,128]{1,0:T(8,128)(2,1)S(1)}, bf16[224,128]{1,0:T(8,128)(2,1)S(1)}, u32[]{:S(2)}, u32[]{:S(2)}) %collective-permute-start.6) | collective-permute-done | bytes 57376 | tf_op jit(solution)/shard_map/ppermute | solution.py:258
  24.3 2.4 %collective-permute-done.5 = bf16[224,128]{1,0:T(8,128)(2,1)S(1)} collective-permute-done((bf16[224,128]{1,0:T(8,128)(2,1)S(1)}, bf16[224,128]{1,0:T(8,128)(2,1)S(1)}, u32[]{:S(2)}, u32[]{:S(2)}) %collective-permute-start.5) | collective-permute-done | bytes 57376 | tf_op jit(solution)/shard_map/ppermute | solution.py:258
  26.7 0.2 collective-permute-done.4
  27.0 1.1 %collective-permute-start.7 = (bf16[224,128]{1,0:T(8,128)(2,1)S(1)}, bf16[224,128]{1,0:T(8,128)(2,1)S(1)}, u32[]{:S(2)}, u32[]{:S(2)}) collective-permute-start(bf16[224,128]{1,0:T(8,128)(2,1)S(1)} %add_convert_fusion.near0), channel_id=1, source_target_pairs={{0,8},{1,9},{2,10},{3,11},{4,12},{5,13},{6,14},{7,15},{8,0},{9,1},... | collective-permute-start | bytes 172040 | tf_op jit(solution)/shard_map/ppermute | solution.py:258
  28.1 0.9 %collective-permute-start.8 = (bf16[224,128]{1,0:T(8,128)(2,1)S(1)}, bf16[224,128]{1,0:T(8,128)(2,1)S(1)}, u32[]{:S(2)}, u32[]{:S(2)}) collective-permute-start(bf16[224,128]{1,0:T(8,128)(2,1)S(1)} %add_convert_fusion.near0), channel_id=1, source_target_pairs={{0,16},{1,17},{2,18},{3,19},{4,20},{5,21},{6,22},{7,23},{8,24},{9,... | collective-permute-start | bytes 172040 | tf_op jit(solution)/shard_map/ppermute | solution.py:258
  28.9 1.6 %collective-permute-start.9 = (bf16[224,128]{1,0:T(8,128)(2,1)S(1)}, bf16[224,128]{1,0:T(8,128)(2,1)S(1)}, u32[]{:S(2)}, u32[]{:S(2)}) collective-permute-start(bf16[224,128]{1,0:T(8,128)(2,1)S(1)} %add_convert_fusion.near0), channel_id=1, source_target_pairs={{0,24},{1,25},{2,26},{3,27},{4,28},{5,29},{6,30},{7,31},{8,16},{9,... | collective-permute-start | bytes 172040 | tf_op jit(solution)/shard_map/ppermute | solution.py:258
  30.5 0.8 %collective-permute-done.7.near1 = bf16[224,128]{1,0:T(8,128)(2,1)S(1)} collective-permute-done((bf16[224,128]{1,0:T(8,128)(2,1)S(1)}, bf16[224,128]{1,0:T(8,128)(2,1)S(1)}, u32[]{:S(2)}, u32[]{:S(2)}) %collective-permute-start.7) | collective-permute-done | bytes 57376 | tf_op jit(solution)/shard_map/ppermute | solution.py:258
  31.4 0.8 %collective-permute-done.8.near2 = bf16[224,128]{1,0:T(8,128)(2,1)S(1)} collective-permute-done((bf16[224,128]{1,0:T(8,128)(2,1)S(1)}, bf16[224,128]{1,0:T(8,128)(2,1)S(1)}, u32[]{:S(2)}, u32[]{:S(2)}) %collective-permute-start.8) | collective-permute-done | bytes 57376 | tf_op jit(solution)/shard_map/ppermute | solution.py:258
  32.2 1.8 %collective-permute-done.9.near3 = bf16[224,128]{1,0:T(8,128)(2,1)S(1)} collective-permute-done((bf16[224,128]{1,0:T(8,128)(2,1)S(1)}, bf16[224,128]{1,0:T(8,128)(2,1)S(1)}, u32[]{:S(2)}, u32[]{:S(2)}) %collective-permute-start.9) | collective-permute-done | bytes 57376 | tf_op jit(solution)/shard_map/ppermute | solution.py:258
  34.0 0.1 collective-permute-start.10
  34.1 1.5 %collective-permute-done.10.far_ref = bf16[896,128]{1,0:T(8,128)(2,1)S(1)} collective-permute-done((bf16[896,128]{1,0:T(8,128)(2,1)S(1)}, bf16[896,128]{1,0:T(8,128)(2,1)S(1)}, u32[]{:S(2)}, u32[]{:S(2)}) %collective-permute-start.10) | collective-permute-done | bytes 229408 | tf_op jit(solution)/shard_map/ppermute | solution.py:258
  35.6 1.1 %clip.1 = (bf16[288,384]{1,0:T(8,128)(2,1)}, bf16[384]{0:T(512)(128)(2,1)}, bf16[288,384]{1,0:T(8,128)(2,1)}, bf16[288]{0:T(512)(128)(2,1)}, bf16[768]{0:T(1024)(128)(2,1)}, /*index=5*/bf16[768]{0:T(1024)(128)(2,1)}) custom-call(s32[1]{0:T(128)} %bitcast.me_ref, bf16[224,128]{1,0:T(8,128)(2,1)S(1)} %add_convert_fusion.near0, ...), custom_call_target="tpu_custom_call" | custom-call | tf_op jit(solution)/shard_map/clip/pallas_call | solution.py:353
  (5 shorter events, 0.2 us)
Async XLA Ops:
  7.4 2.8 %collective-permute-start = (bf16[896,128]{1,0:T(8,128)(2,1)S(1)}, bf16[896,128]{1,0:T(8,128)(2,1)S(1)}, u32[]{:S(2)}, u32[]{:S(2)}) collective-permute-start(bf16[896,128]{1,0:T(8,128)(2,1)S(1)} %get-tuple-element.18), channel_id=1, source_target_pairs={{0,4},{1,5},{2,6},{3,7},{4,0},{5,1},{6,2},{7,3},{8,12},{9,13},{10,... | collective-permute-start | bytes 688136 | tf_op jit(solution)/shard_map/ppermute | solution.py:258
  10.3 5.2 %collective-permute-start.3 = (bf16[224,128]{1,0:T(8,128)(2,1)S(1)}, bf16[224,128]{1,0:T(8,128)(2,1)S(1)}, u32[]{:S(2)}, u32[]{:S(2)}) collective-permute-start(bf16[224,128]{1,0:T(8,128)(2,1)S(1)} %get-tuple-element.26), channel_id=1, source_target_pairs={{0,24},{1,25},{2,26},{3,27},{4,28},{5,29},{6,30},{7,31},{8,16},{9,... | collective-permute-start | bytes 172040 | tf_op jit(solution)/shard_map/ppermute | solution.py:258
  13.0 4.2 %collective-permute-start.2 = (bf16[224,128]{1,0:T(8,128)(2,1)S(1)}, bf16[224,128]{1,0:T(8,128)(2,1)S(1)}, u32[]{:S(2)}, u32[]{:S(2)}) collective-permute-start(bf16[224,128]{1,0:T(8,128)(2,1)S(1)} %get-tuple-element.27), channel_id=1, source_target_pairs={{0,16},{1,17},{2,18},{3,19},{4,20},{5,21},{6,22},{7,23},{8,24},{9,... | collective-permute-start | bytes 172040 | tf_op jit(solution)/shard_map/ppermute | solution.py:258
  13.7 4.3 %collective-permute-start.1 = (bf16[224,128]{1,0:T(8,128)(2,1)S(1)}, bf16[224,128]{1,0:T(8,128)(2,1)S(1)}, u32[]{:S(2)}, u32[]{:S(2)}) collective-permute-start(bf16[224,128]{1,0:T(8,128)(2,1)S(1)} %get-tuple-element.25), channel_id=1, source_target_pairs={{0,8},{1,9},{2,10},{3,11},{4,12},{5,13},{6,14},{7,15},{8,0},{9,1},... | collective-permute-start | bytes 172040 | tf_op jit(solution)/shard_map/ppermute | solution.py:258
  18.0 6.3 %collective-permute-start.6 = (bf16[224,128]{1,0:T(8,128)(2,1)S(1)}, bf16[224,128]{1,0:T(8,128)(2,1)S(1)}, u32[]{:S(2)}, u32[]{:S(2)}) collective-permute-start(bf16[224,128]{1,0:T(8,128)(2,1)S(1)} %add_convert_fusion.1), channel_id=1, source_target_pairs={{0,3},{1,2},{2,1},{3,0},{4,7},{5,6},{6,5},{7,4},{8,11},{9,10},{10,... | collective-permute-start | bytes 172040 | tf_op jit(solution)/shard_map/ppermute | solution.py:258
  21.1 5.6 %collective-permute-start.5 = (bf16[224,128]{1,0:T(8,128)(2,1)S(1)}, bf16[224,128]{1,0:T(8,128)(2,1)S(1)}, u32[]{:S(2)}, u32[]{:S(2)}) collective-permute-start(bf16[224,128]{1,0:T(8,128)(2,1)S(1)} %add_convert_fusion.1), channel_id=1, source_target_pairs={{0,2},{1,3},{2,0},{3,1},{4,6},{5,7},{6,4},{7,5},{8,10},{9,11},{10,... | collective-permute-start | bytes 172040 | tf_op jit(solution)/shard_map/ppermute | solution.py:258
  22.2 4.8 %collective-permute-start.4 = (bf16[224,128]{1,0:T(8,128)(2,1)S(1)}, bf16[224,128]{1,0:T(8,128)(2,1)S(1)}, u32[]{:S(2)}, u32[]{:S(2)}) collective-permute-start(bf16[224,128]{1,0:T(8,128)(2,1)S(1)} %add_convert_fusion.1), channel_id=1, source_target_pairs={{0,1},{1,0},{2,3},{3,2},{4,5},{5,4},{6,7},{7,6},{8,9},{9,8},{10,11... | collective-permute-start | bytes 172040 | tf_op jit(solution)/shard_map/ppermute | solution.py:258
  27.0 4.4 %collective-permute-start.7 = (bf16[224,128]{1,0:T(8,128)(2,1)S(1)}, bf16[224,128]{1,0:T(8,128)(2,1)S(1)}, u32[]{:S(2)}, u32[]{:S(2)}) collective-permute-start(bf16[224,128]{1,0:T(8,128)(2,1)S(1)} %add_convert_fusion.near0), channel_id=1, source_target_pairs={{0,8},{1,9},{2,10},{3,11},{4,12},{5,13},{6,14},{7,15},{8,0},{9,1},... | collective-permute-start | bytes 172040 | tf_op jit(solution)/shard_map/ppermute | solution.py:258
  28.1 4.2 %collective-permute-start.8 = (bf16[224,128]{1,0:T(8,128)(2,1)S(1)}, bf16[224,128]{1,0:T(8,128)(2,1)S(1)}, u32[]{:S(2)}, u32[]{:S(2)}) collective-permute-start(bf16[224,128]{1,0:T(8,128)(2,1)S(1)} %add_convert_fusion.near0), channel_id=1, source_target_pairs={{0,16},{1,17},{2,18},{3,19},{4,20},{5,21},{6,22},{7,23},{8,24},{9,... | collective-permute-start | bytes 172040 | tf_op jit(solution)/shard_map/ppermute | solution.py:258
  28.9 5.1 %collective-permute-start.9 = (bf16[224,128]{1,0:T(8,128)(2,1)S(1)}, bf16[224,128]{1,0:T(8,128)(2,1)S(1)}, u32[]{:S(2)}, u32[]{:S(2)}) collective-permute-start(bf16[224,128]{1,0:T(8,128)(2,1)S(1)} %add_convert_fusion.near0), channel_id=1, source_target_pairs={{0,24},{1,25},{2,26},{3,27},{4,28},{5,29},{6,30},{7,31},{8,16},{9,... | collective-permute-start | bytes 172040 | tf_op jit(solution)/shard_map/ppermute | solution.py:258
  34.0 1.6 %collective-permute-start.10 = (bf16[896,128]{1,0:T(8,128)(2,1)S(1)}, bf16[896,128]{1,0:T(8,128)(2,1)S(1)}, u32[]{:S(2)}, u32[]{:S(2)}) collective-permute-start(bf16[896,128]{1,0:T(8,128)(2,1)S(1)} %pad_maximum_fusion), channel_id=1, source_target_pairs={{0,4},{1,5},{2,6},{3,7},{4,0},{5,1},{6,2},{7,3},{8,12},{9,13},{10,... | collective-permute-start | bytes 688136 | tf_op jit(solution)/shard_map/ppermute | solution.py:258

commit v3 on v2

--- a/solution.py
+++ b/solution.py
@@ -8,8 +8,10 @@
 from jax.experimental.pallas import tpu as pltpu
 from jax.sharding import PartitionSpec as P
 
+
 TILE = 32
 LANES = 128
+VMEM_LIMIT = 24 * 2**20
 AXES = ("dp", "group")
 ln_epsilon = 1e-05
 clip_share = 0.5
@@ -47,6 +49,22 @@
 def grad_kernel(
     pair,
     me_ref,
+    tiles_hbm,
+    patches_hbm,
+    tok_hbm,
+    cot_hbm,
+    mask_hbm,
+    w_in_hbm,
+    b_in_hbm,
+    w_out_hbm,
+    gain_hbm,
+    shift_hbm,
+    keep_ref,
+    send_ref,
+    dn_s,
+    alive_s,
+    mean_s,
+    inv_s,
     tiles_ref,
     patches_ref,
     tok_ref,
@@ -57,24 +75,42 @@
     w_out_ref,
     gain_ref,
     shift_ref,
-    dtok_ref,
-    keep_ref,
-    send_ref,
-    flat_ref,
     y_s,
     o_s,
-    dn_s,
     w_in_t,
     w_out_s,
     bias_s,
-    alive_s,
-    mean_s,
-    inv_s,
     gin_s,
     gout_s,
     bin_s,
     bout_s,
+    sems,
 ):
+    sources = (tiles_hbm, patches_hbm, mask_hbm, gain_hbm, shift_hbm, b_in_hbm)
+    targets = (tiles_ref, patches_ref, mask_ref, gain_ref, shift_ref, b_in_ref)
+    copies = [
+        pltpu.make_async_copy(source, target, sems.at[i])
+        for i, (source, target) in enumerate(zip(sources, targets))
+    ]
+    fetch_tok = pltpu.make_async_copy(tok_hbm, tok_ref, sems.at[6])
+    fetch_cot = pltpu.make_async_copy(cot_hbm, cot_ref, sems.at[7])
+    fetch_in = pltpu.make_async_copy(w_in_hbm, w_in_ref, sems.at[8])
+    fetch_out = pltpu.make_async_copy(w_out_hbm, w_out_ref, sems.at[9])
+    for copy in copies:
+        copy.start()
+    for copy in (fetch_tok, fetch_cot, fetch_in, fetch_out):
+        copy.start()
+    gin_s[...] = jnp.zeros(gin_s.shape, f32)
+    gout_s[...] = jnp.zeros(gout_s.shape, f32)
+    bin_s[...] = jnp.zeros(bin_s.shape, f32)
+    bout_s[...] = jnp.zeros(bout_s.shape, f32)
+    tail = slice(tok_ref.shape[0], y_s.shape[0])
+    y_s[tail, :] = jnp.zeros((w_in_ref.shape[0], tok_ref.shape[1]), bf16)
+    o_s[tail, :] = jnp.zeros((w_in_ref.shape[0], tok_ref.shape[1]), bf16)
+    for copy in copies:
+        copy.wait()
+    fetch_tok.wait()
+    fetch_cot.wait()
     rows, width = tok_ref.shape
     places, hidden = w_in_ref.shape
     slots = tiles_ref.shape[0]
@@ -86,14 +122,6 @@
     side = (me // pair) % 2
     gain = gain_ref[...].reshape(1, width)
     shift = shift_ref[...].reshape(1, width)
-
-    w_in_t[...] = jnp.transpose(w_in_ref[...])
-    w_out_s[...] = jnp.transpose(w_out_ref[...])
-    bias_s[...] = as_column(b_in_ref[...].reshape(1, hidden))
-    gin_s[...] = jnp.zeros(gin_s.shape, f32)
-    gout_s[...] = jnp.zeros(gout_s.shape, f32)
-    bin_s[...] = jnp.zeros(bin_s.shape, f32)
-    bout_s[...] = jnp.zeros(bout_s.shape, f32)
 
     mask_row = mask_ref[...].astype(f32).reshape(1, rows)
     short = -rows % LANES
@@ -117,9 +145,11 @@
         alive = alive_s[piece, :1]
         y_s[piece, :] = ((center * inv_std * gain + shift) * alive).astype(bf16)
         o_s[piece, :] = (cot_ref[piece, :].astype(f32) * alive).astype(bf16)
-    tail = slice(rows, y_s.shape[0])
-    y_s[tail, :] = jnp.zeros((places, width), bf16)
-    o_s[tail, :] = jnp.zeros((places, width), bf16)
+    fetch_in.wait()
+    fetch_out.wait()
+    w_in_t[...] = jnp.transpose(w_in_ref[...])
+    w_out_s[...] = jnp.transpose(w_out_ref[...])
+    bias_s[...] = as_column(b_in_ref[...].reshape(1, hidden))
 
     chunk = 256
     third = places // 3
@@ -178,33 +208,50 @@
         scaled_x = d_rows * normal_x
         gain_sum += jnp.sum(scaled_x.reshape(step // 8, 8, width), axis=0)
         shift_sum += jnp.sum(d_rows.reshape(step // 8, 8, width), axis=0)
-        scaled = d_rows * gain
-        middle = row_total(scaled) * (1.0 / width)
-        inner = row_total(scaled_x * gain) * (1.0 / width)
-        d_norm = (scaled - middle - normal_x * inner) * inv_std
-        dtok_ref[piece, :] = (cot_ref[piece, :].astype(f32) + d_norm).astype(bf16)
 
     blocks = hidden // LANES
     small = blocks * places
-    pairs = (
+    parts = (
         (gin_s, bin_s[...], gain_sum),
         (gout_s, bout_s[...], shift_sum),
     )
-    for which, (weights, bias_part, wide_part) in enumerate(pairs):
-        base = which * half
+
+    def write(ref, weights, bias_part, wide_part):
         for j in range(blocks):
-            flat_ref[base + j * places : base + (j + 1) * places, :] = weights[
+            ref[j * places : (j + 1) * places, :] = weights[
                 :, j * LANES : (j + 1) * LANES
-            ]
-        flat_ref[base + small : base + half, :] = jnp.zeros((half - small, LANES), f32)
+            ].astype(ref.dtype)
         bias_row = jnp.sum(jnp.transpose(bias_part), axis=0, keepdims=True)
         wide_row = jnp.sum(wide_part, axis=0, keepdims=True)
-        at = base + small
-        for block in lane_blocks(bias_row) + lane_blocks(wide_row):
-            flat_ref[at : at + 1, :] = block
-            at += 1
-    keep_ref[...] = flat_ref[pl.ds(pl.multiple_of(side * half, 16), half), :]
-    send_ref[...] = flat_ref[pl.ds(pl.multiple_of((1 - side) * half, 16), half), :].astype(bf16)
+        rest = lane_blocks(bias_row) + lane_blocks(wide_row)
+        rest.append(jnp.zeros((half - small - len(rest), LANES), f32))
+        ref[small:half, :] = jnp.concatenate(rest, axis=0).astype(ref.dtype)
+
+    for which in (0, 1):
+
+        @pl.when(side == which)
+        def _():
+            write(keep_ref, *parts[which])
+            write(send_ref, *parts[1 - which])
+
+
+def token_kernel(
+    tok_ref, cot_ref, gain_ref, dn_ref, alive_s, mean_s, inv_s, dtok_ref
+):
+    rows, width = tok_ref.shape
+    gain = gain_ref[...].reshape(1, width)
+    step = 64
+    for at in range(0, rows, step):
+        piece = slice(at, at + step)
+        alive = alive_s[piece, :1]
+        inv_std = inv_s[piece, :1]
+        normal_x = (tok_ref[piece, :].astype(f32) - mean_s[piece, :1]) * inv_std
+        d_rows = jnp.where(alive > 0.0, dn_ref[piece, :].astype(f32), 0.0)
+        scaled = d_rows * gain
+        middle = row_total(scaled) * (1.0 / width)
+        inner = row_total(scaled * normal_x) * (1.0 / width)
+        d_norm = (scaled - middle - normal_x * inner) * inv_std
+        dtok_ref[piece, :] = (cot_ref[piece, :].astype(f32) + d_norm).astype(bf16)
 
 
 def all_terms(pair, me, tokens, cotangent, mask, image_tiles, patches, w_in, b_in, w_out, gain, shift):
@@ -213,45 +260,71 @@
     half = half_rows(places, hidden, width)
     smem = pl.BlockSpec(memory_space=pltpu.SMEM)
     vmem = pl.BlockSpec(memory_space=pltpu.VMEM)
-    return pl.pallas_call(
+    anywhere = pl.BlockSpec(memory_space=pltpu.HBM)
+    keep, send, dn, alive, mean, inv_std = pl.pallas_call(
         functools.partial(grad_kernel, pair),
         name="terms",
         out_shape=(
-            jax.ShapeDtypeStruct((rows, width), bf16),
             pltpu.VMEM((half, LANES), f32),
             pltpu.VMEM((half, LANES), bf16),
+            pltpu.VMEM((rows + places, width), bf16),
+            pltpu.VMEM((rows, LANES), f32),
+            pltpu.VMEM((rows, LANES), f32),
+            pltpu.VMEM((rows, LANES), f32),
         ),
-        in_specs=[smem] * 3 + [vmem] * 8,
-        out_specs=(vmem, vmem, vmem),
+        in_specs=[smem] + [anywhere] * 10,
+        out_specs=(vmem,) * 6,
         scratch_shapes=[
-            pltpu.VMEM((2 * half, LANES), f32),
-            pltpu.VMEM((rows + places, width), bf16),
+            pltpu.SMEM(image_tiles.shape[::-1], jnp.int32),
+            pltpu.SMEM(patches.shape[::-1], jnp.int32),
+            pltpu.VMEM((rows, width), bf16),
+            pltpu.VMEM((rows, width), bf16),
+            pltpu.VMEM((rows,), jnp.int32),
+            pltpu.VMEM((places, hidden), bf16),
+            pltpu.VMEM((hidden,), f32),
+            pltpu.VMEM((places, hidden), bf16),
+            pltpu.VMEM((width,), f32),
+            pltpu.VMEM((width,), f32),
             pltpu.VMEM((rows + places, width), bf16),
             pltpu.VMEM((rows + places, width), bf16),
             pltpu.VMEM((hidden, places), bf16),
             pltpu.VMEM((hidden, places), bf16),
             pltpu.VMEM((hidden, LANES), f32),
-            pltpu.VMEM((rows, LANES), f32),
-            pltpu.VMEM((rows, LANES), f32),
-            pltpu.VMEM((rows, LANES), f32),
             pltpu.VMEM((places, hidden), f32),
             pltpu.VMEM((places, hidden), f32),
             pltpu.VMEM((hidden, LANES), f32),
             pltpu.VMEM((hidden, LANES), f32),
+            pltpu.SemaphoreType.DMA((10,)),
         ],
+        compiler_params=pltpu.CompilerParams(vmem_limit_bytes=VMEM_LIMIT),
     )(
         me.reshape(1),
-        image_tiles.T,
-        patches.T,
-        tokens,
-        cotangent,
-        mask,
-        w_in,
-        b_in,
-        w_out.T,
-        gain,
-        shift,
+        *[
+            pltpu.with_memory_space_constraint(x, pltpu.HBM)
+            for x in (
+                image_tiles.T,
+                patches.T,
+                tokens,
+                cotangent,
+                mask,
+                w_in,
+                b_in,
+                w_out.T,
+                gain,
+                shift,
+            )
+        ],
     )
+    kept = [pltpu.with_memory_space_constraint(x, pltpu.VMEM) for x in (dn, alive, mean, inv_std)]
+    dtokens = pl.pallas_call(
+        token_kernel,
+        name="rows",
+        out_shape=jax.ShapeDtypeStruct((rows, width), bf16),
+        in_specs=[vmem] * 7,
+        out_specs=vmem,
+        compiler_params=pltpu.CompilerParams(vmem_limit_bytes=VMEM_LIMIT),
+    )(tokens, cotangent, gain, *kept)
+    return dtokens, keep, send
 
 
 def swap(x, mask, devices):
@@ -279,13 +352,13 @@
     rest = [1 << b for b in range(devices.bit_length() - 1)]
     rest = [m for m in rest if m not in (pair, plane, 2 * plane)]
     while rest:
-        if len(rest) > 1:
-            low, high = rest[:2]
-            rest = rest[2:]
-            others = [swap(own, m, devices).astype(f32) for m in (low, high, low + high)]
-            own = (own.astype(f32) + others[0]) + (others[1] + others[2])
-        else:
-            own = own.astype(f32) + swap(own, rest.pop(), devices).astype(f32)
+        low, high = (rest + [0])[:2]
+        rest = rest[2:]
+        masks = [low, high, low + high] if high else [low]
+        others = [swap(own, m, devices).astype(f32) for m in masks]
+        own = own.astype(f32) + others[0]
+        if high:
+            own = own + (others[1] + others[2])
         own = own.astype(bf16)
     near = [own] + [swap(own, k * plane, devices) for k in (1, 2, 3)]
     return near, swap(jnp.concatenate(near), pair, devices)

time: 37.2 us -> 38.2 us (1.027)
  starting transfers between devices: 14.1 us -> 16.2 us
  Pallas kernels: 7.89 us -> 5.82 us
  waiting for transfers between devices: 13.8 us -> 14.5 us
  local copies, waits for them, and re-layouts: 0.04 us -> 0.63 us
    pallas_call x1, Pallas kernels: 6.79 us -> 3.12 us  [all_terms(): pl.pallas_call(functools.partial(grad_kernel, pair), name='terms', out_sh...]
    ppermute x11, starting transfers between devices: 14.1 us -> 16.2 us  [swap(): return lax.ppermute(x, AXES, [(i, i ^ mask) for i in range(devices)])]
    pallas_call x0 -> x1, Pallas kernels: none -> 1.6 us  [all_terms(): pl.pallas_call(token_kernel, name='rows', out_shape=jax.ShapeDtypeStruct(...]
    ppermute x11, waiting for transfers between devices: 13.8 us -> 14.5 us  [swap(): return lax.ppermute(x, AXES, [(i, i ^ mask) for i in range(devices)])]
    unnamed x0 -> x6, local copies, waits for them, and re-layouts: none -> 0.59 us
  transfers between devices with their start and end apart: 11 -> 11, of which waited for: 11 -> 10; matrix products, arithmetic and copies ran while one was open for 0% -> 0% of each run, Pallas kernels for 0% -> 4%
where the time goes in v3:
time: 38.2 us; the launch traced here: 38 us
  starting transfers between devices  16.2 us (42%)
  waiting for transfers between devices  14.5 us (38%)
  Pallas kernels  5.82 us (15%)
  between operations  0.72 us (2%)
  local copies, waits for them, and re-layouts  0.63 us (2%)
    ppermute x11, starting transfers between devices, swap(): return lax.ppermute(x, AXES, [(i, i ^ mask) for i in range(devices)])  16.2 us
    ppermute x11, waiting for transfers between devices, swap(): return lax.ppermute(x, AXES, [(i, i ^ mask) for i in range(devices)])  14.5 us
    pallas_call x1, Pallas kernels, all_terms(): pl.pallas_call(functools.partial(grad_kernel, pair), name='terms', out_sh...  3.12 us
    pallas_call x1, Pallas kernels, all_terms(): pl.pallas_call(token_kernel, name='rows', out_shape=jax.ShapeDtypeStruct(...  1.6 us
    pallas_call x1, Pallas kernels, clipped(): pl.pallas_call(functools.partial(clip_kernel, pair), name='clip', out_sha...  1.11 us
  transfers between devices with their start and end apart: 11, of which 10 were waited for; matrix products, arithmetic and copies ran while one was open for 0% of the time, Pallas kernels for 4%

profile of v3, /device:TPU:0, one launch (start us, length us, event | category | flops | bytes accessed | tf_op | source)
XLA Modules:
  0.0 38.0 jit_solution(1814547313159490891)
XLA Ops:
  0.6 3.1 %terms.1 = (f32[896,128]{1,0:T(8,128)S(1)}, bf16[896,128]{1,0:T(8,128)(2,1)S(1)}, bf16[608,768]{1,0:T(8,128)(2,1)S(1)}, f32[320,128]{1,0:T(8,128)S(1)}, f32[320,128]{1,0:T(8,128)S(1)}, /*index=5*/f32[320,128]{1,0:T(8,128)S(1)}) custom-call(s32[1]{0:T(128)} %bitcast.me_ref, s32[3,32]{1,0:T(4,128)} %bitcast.6, s32[3,32]{1,0:T(4,128)} %bitcast.7, ...), custom_call_target="tpu_custom_call" | custom-call | tf_op jit(solution)/shard_map/terms/pallas_call | solution.py:264
  3.8 2.9 %collective-permute-start = (bf16[896,128]{1,0:T(8,128)(2,1)S(1)}, bf16[896,128]{1,0:T(8,128)(2,1)S(1)}, u32[]{:S(2)}, u32[]{:S(2)}) collective-permute-start(bf16[896,128]{1,0:T(8,128)(2,1)S(1)} %get-tuple-element.24), channel_id=1, source_target_pairs={{0,4},{1,5},{2,6},{3,7},{4,0},{5,1},{6,2},{7,3},{8,12},{9,13},{10,... | collective-permute-start | bytes 688136 | tf_op jit(solution)/shard_map/ppermute | solution.py:331
  6.7 1.1 %collective-permute-done = bf16[896,128]{1,0:T(8,128)(2,1)S(1)} collective-permute-done((bf16[896,128]{1,0:T(8,128)(2,1)S(1)}, bf16[896,128]{1,0:T(8,128)(2,1)S(1)}, u32[]{:S(2)}, u32[]{:S(2)}) %collective-permute-start) | collective-permute-done | bytes 229408 | tf_op jit(solution)/shard_map/ppermute | solution.py:331
  7.9 2.9 %collective-permute-start.1 = (bf16[224,128]{1,0:T(8,128)(2,1)S(1)}, bf16[224,128]{1,0:T(8,128)(2,1)S(1)}, u32[]{:S(2)}, u32[]{:S(2)}) collective-permute-start(bf16[224,128]{1,0:T(8,128)(2,1)S(1)} %get-tuple-element.31), channel_id=1, source_target_pairs={{0,8},{1,9},{2,10},{3,11},{4,12},{5,13},{6,14},{7,15},{8,0},{9,1},... | collective-permute-start | bytes 172040 | tf_op jit(solution)/shard_map/ppermute | solution.py:331
  10.8 1.5 %collective-permute-start.2 = (bf16[224,128]{1,0:T(8,128)(2,1)S(1)}, bf16[224,128]{1,0:T(8,128)(2,1)S(1)}, u32[]{:S(2)}, u32[]{:S(2)}) collective-permute-start(bf16[224,128]{1,0:T(8,128)(2,1)S(1)} %get-tuple-element.33), channel_id=1, source_target_pairs={{0,16},{1,17},{2,18},{3,19},{4,20},{5,21},{6,22},{7,23},{8,24},{9,... | collective-permute-start | bytes 172040 | tf_op jit(solution)/shard_map/ppermute | solution.py:331
  12.3 0.0 collective-permute-start.3
  12.3 0.0 copy-start
  12.3 0.0 copy-start.1
  12.3 0.7 %collective-permute-done.1 = bf16[224,128]{1,0:T(8,128)(2,1)S(1)} collective-permute-done((bf16[224,128]{1,0:T(8,128)(2,1)S(1)}, bf16[224,128]{1,0:T(8,128)(2,1)S(1)}, u32[]{:S(2)}, u32[]{:S(2)}) %collective-permute-start.1) | collective-permute-done | bytes 57376 | tf_op jit(solution)/shard_map/ppermute | solution.py:331
  13.0 2.0 %collective-permute-done.2 = bf16[224,128]{1,0:T(8,128)(2,1)S(1)} collective-permute-done((bf16[224,128]{1,0:T(8,128)(2,1)S(1)}, bf16[224,128]{1,0:T(8,128)(2,1)S(1)}, u32[]{:S(2)}, u32[]{:S(2)}) %collective-permute-start.2) | collective-permute-done | bytes 57376 | tf_op jit(solution)/shard_map/ppermute | solution.py:331
  15.0 2.4 %collective-permute-done.3 = bf16[224,128]{1,0:T(8,128)(2,1)S(1)} collective-permute-done((bf16[224,128]{1,0:T(8,128)(2,1)S(1)}, bf16[224,128]{1,0:T(8,128)(2,1)S(1)}, u32[]{:S(2)}, u32[]{:S(2)}) %collective-permute-start.3) | collective-permute-done | bytes 57376 | tf_op jit(solution)/shard_map/ppermute | solution.py:331
  17.4 2.8 %collective-permute-start.4 = (bf16[224,128]{1,0:T(8,128)(2,1)S(1)}, bf16[224,128]{1,0:T(8,128)(2,1)S(1)}, u32[]{:S(2)}, u32[]{:S(2)}) collective-permute-start(bf16[224,128]{1,0:T(8,128)(2,1)S(1)} %add_convert_fusion.1), channel_id=1, source_target_pairs={{0,1},{1,0},{2,3},{3,2},{4,5},{5,4},{6,7},{7,6},{8,9},{9,8},{10,11... | collective-permute-start | bytes 172040 | tf_op jit(solution)/shard_map/ppermute | solution.py:331
  20.2 1.2 %collective-permute-start.5 = (bf16[224,128]{1,0:T(8,128)(2,1)S(1)}, bf16[224,128]{1,0:T(8,128)(2,1)S(1)}, u32[]{:S(2)}, u32[]{:S(2)}) collective-permute-start(bf16[224,128]{1,0:T(8,128)(2,1)S(1)} %add_convert_fusion.1), channel_id=1, source_target_pairs={{0,2},{1,3},{2,0},{3,1},{4,6},{5,7},{6,4},{7,5},{8,10},{9,11},{10,... | collective-permute-start | bytes 172040 | tf_op jit(solution)/shard_map/ppermute | solution.py:331
  21.4 1.3 %collective-permute-start.6 = (bf16[224,128]{1,0:T(8,128)(2,1)S(1)}, bf16[224,128]{1,0:T(8,128)(2,1)S(1)}, u32[]{:S(2)}, u32[]{:S(2)}) collective-permute-start(bf16[224,128]{1,0:T(8,128)(2,1)S(1)} %add_convert_fusion.1), channel_id=1, source_target_pairs={{0,3},{1,2},{2,1},{3,0},{4,7},{5,6},{6,5},{7,4},{8,11},{9,10},{10,... | collective-permute-start | bytes 172040 | tf_op jit(solution)/shard_map/ppermute | solution.py:331
  22.7 0.3 collective-permute-done.4
  23.0 3.0 %collective-permute-done.5 = bf16[224,128]{1,0:T(8,128)(2,1)S(1)} collective-permute-done((bf16[224,128]{1,0:T(8,128)(2,1)S(1)}, bf16[224,128]{1,0:T(8,128)(2,1)S(1)}, u32[]{:S(2)}, u32[]{:S(2)}) %collective-permute-start.5) | collective-permute-done | bytes 57376 | tf_op jit(solution)/shard_map/ppermute | solution.py:331
  26.0 1.3 %collective-permute-done.6 = bf16[224,128]{1,0:T(8,128)(2,1)S(1)} collective-permute-done((bf16[224,128]{1,0:T(8,128)(2,1)S(1)}, bf16[224,128]{1,0:T(8,128)(2,1)S(1)}, u32[]{:S(2)}, u32[]{:S(2)}) %collective-permute-start.6) | collective-permute-done | bytes 57376 | tf_op jit(solution)/shard_map/ppermute | solution.py:331
  27.4 2.0 %collective-permute-start.7 = (bf16[224,128]{1,0:T(8,128)(2,1)S(1)}, bf16[224,128]{1,0:T(8,128)(2,1)S(1)}, u32[]{:S(2)}, u32[]{:S(2)}) collective-permute-start(bf16[224,128]{1,0:T(8,128)(2,1)S(1)} %add_convert_fusion.near0), channel_id=1, source_target_pairs={{0,8},{1,9},{2,10},{3,11},{4,12},{5,13},{6,14},{7,15},{8,0},{9,1},... | collective-permute-start | bytes 172040 | tf_op jit(solution)/shard_map/ppermute | solution.py:331
  29.4 0.1 collective-permute-start.8
  29.5 1.4 %collective-permute-start.9 = (bf16[224,128]{1,0:T(8,128)(2,1)S(1)}, bf16[224,128]{1,0:T(8,128)(2,1)S(1)}, u32[]{:S(2)}, u32[]{:S(2)}) collective-permute-start(bf16[224,128]{1,0:T(8,128)(2,1)S(1)} %add_convert_fusion.near0), channel_id=1, source_target_pairs={{0,24},{1,25},{2,26},{3,27},{4,28},{5,29},{6,30},{7,31},{8,16},{9,... | collective-permute-start | bytes 172040 | tf_op jit(solution)/shard_map/ppermute | solution.py:331
  31.0 0.7 %collective-permute-done.7.near1 = bf16[224,128]{1,0:T(8,128)(2,1)S(1)} collective-permute-done((bf16[224,128]{1,0:T(8,128)(2,1)S(1)}, bf16[224,128]{1,0:T(8,128)(2,1)S(1)}, u32[]{:S(2)}, u32[]{:S(2)}) %collective-permute-start.7) | collective-permute-done | bytes 57376 | tf_op jit(solution)/shard_map/ppermute | solution.py:331
  31.7 1.9 %collective-permute-done.8.near2 = bf16[224,128]{1,0:T(8,128)(2,1)S(1)} collective-permute-done((bf16[224,128]{1,0:T(8,128)(2,1)S(1)}, bf16[224,128]{1,0:T(8,128)(2,1)S(1)}, u32[]{:S(2)}, u32[]{:S(2)}) %collective-permute-start.8) | collective-permute-done | bytes 57376 | tf_op jit(solution)/shard_map/ppermute | solution.py:331
  33.6 1.0 %collective-permute-done.9.near3 = bf16[224,128]{1,0:T(8,128)(2,1)S(1)} collective-permute-done((bf16[224,128]{1,0:T(8,128)(2,1)S(1)}, bf16[224,128]{1,0:T(8,128)(2,1)S(1)}, u32[]{:S(2)}, u32[]{:S(2)}) %collective-permute-start.9) | collective-permute-done | bytes 57376 | tf_op jit(solution)/shard_map/ppermute | solution.py:331
  34.6 0.0 copy-start.2
  34.7 0.1 collective-permute-start.10
  34.7 0.0 copy-done
  34.7 0.0 copy-done.1
  34.8 0.6 %copy-done.2 = f32[768]{0:T(1024)S(1)} copy-done((f32[768]{0:T(1024)S(1)}, f32[768]{0:T(1024)}, u32[]{:S(2)}) %copy-start.2) | copy-done | bytes 3096
  35.3 1.6 %rows.1 = bf16[320,768]{1,0:T(8,128)(2,1)} custom-call(bf16[320,768]{1,0:T(8,128)(2,1)S(1)} %copy-done, bf16[320,768]{1,0:T(8,128)(2,1)S(1)} %copy-done.1, f32[768]{0:T(1024)S(1)} %copy-done.2, bf16[608,768]{1,0:T(8,128)(2,1)S(1)} %get-tuple-element.19.dn_ref, f32[320,128]{1,0:T(8,128)S(1)} %get-tuple-element.20.alive_s, ...), custom_call_target="tpu_custom_call" | custom-call | tf_op jit(solution)/shard_map/rows/pallas_call | solution.py:319
  36.9 0.0 collective-permute-done.10.far_ref
  36.9 1.1 %clip.1 = (bf16[288,384]{1,0:T(8,128)(2,1)}, bf16[384]{0:T(512)(128)(2,1)}, bf16[288,384]{1,0:T(8,128)(2,1)}, bf16[288]{0:T(512)(128)(2,1)}, bf16[768]{0:T(1024)(128)(2,1)}, /*index=5*/bf16[768]{0:T(1024)(128)(2,1)}) custom-call(s32[1]{0:T(128)} %bitcast.me_ref, bf16[224,128]{1,0:T(8,128)(2,1)S(1)} %add_convert_fusion.near0, ...), custom_call_target="tpu_custom_call" | custom-call | tf_op jit(solution)/shard_map/clip/pallas_call | solution.py:426
  (5 shorter events, 0.2 us)
Async XLA Ops:
  3.8 4.0 %collective-permute-start = (bf16[896,128]{1,0:T(8,128)(2,1)S(1)}, bf16[896,128]{1,0:T(8,128)(2,1)S(1)}, u32[]{:S(2)}, u32[]{:S(2)}) collective-permute-start(bf16[896,128]{1,0:T(8,128)(2,1)S(1)} %get-tuple-element.24), channel_id=1, source_target_pairs={{0,4},{1,5},{2,6},{3,7},{4,0},{5,1},{6,2},{7,3},{8,12},{9,13},{10,... | collective-permute-start | bytes 688136 | tf_op jit(solution)/shard_map/ppermute | solution.py:331
  7.9 5.1 %collective-permute-start.1 = (bf16[224,128]{1,0:T(8,128)(2,1)S(1)}, bf16[224,128]{1,0:T(8,128)(2,1)S(1)}, u32[]{:S(2)}, u32[]{:S(2)}) collective-permute-start(bf16[224,128]{1,0:T(8,128)(2,1)S(1)} %get-tuple-element.31), channel_id=1, source_target_pairs={{0,8},{1,9},{2,10},{3,11},{4,12},{5,13},{6,14},{7,15},{8,0},{9,1},... | collective-permute-start | bytes 172040 | tf_op jit(solution)/shard_map/ppermute | solution.py:331
  10.8 4.2 %collective-permute-start.2 = (bf16[224,128]{1,0:T(8,128)(2,1)S(1)}, bf16[224,128]{1,0:T(8,128)(2,1)S(1)}, u32[]{:S(2)}, u32[]{:S(2)}) collective-permute-start(bf16[224,128]{1,0:T(8,128)(2,1)S(1)} %get-tuple-element.33), channel_id=1, source_target_pairs={{0,16},{1,17},{2,18},{3,19},{4,20},{5,21},{6,22},{7,23},{8,24},{9,... | collective-permute-start | bytes 172040 | tf_op jit(solution)/shard_map/ppermute | solution.py:331
  12.3 5.1 %collective-permute-start.3 = (bf16[224,128]{1,0:T(8,128)(2,1)S(1)}, bf16[224,128]{1,0:T(8,128)(2,1)S(1)}, u32[]{:S(2)}, u32[]{:S(2)}) collective-permute-start(bf16[224,128]{1,0:T(8,128)(2,1)S(1)} %get-tuple-element.32), channel_id=1, source_target_pairs={{0,24},{1,25},{2,26},{3,27},{4,28},{5,29},{6,30},{7,31},{8,16},{9,... | collective-permute-start | bytes 172040 | tf_op jit(solution)/shard_map/ppermute | solution.py:331
  12.3 22.4 %copy-start = (bf16[320,768]{1,0:T(8,128)(2,1)S(1)}, bf16[320,768]{1,0:T(8,128)(2,1)}, u32[]{:S(2)}) copy-start(bf16[320,768]{1,0:T(8,128)(2,1)} %tok_ref.1) | copy-start | bytes 1474564
  12.3 22.4 %copy-start.1 = (bf16[320,768]{1,0:T(8,128)(2,1)S(1)}, bf16[320,768]{1,0:T(8,128)(2,1)}, u32[]{:S(2)}) copy-start(bf16[320,768]{1,0:T(8,128)(2,1)} %cot_ref.1) | copy-start | bytes 1474564
  17.4 5.6 %collective-permute-start.4 = (bf16[224,128]{1,0:T(8,128)(2,1)S(1)}, bf16[224,128]{1,0:T(8,128)(2,1)S(1)}, u32[]{:S(2)}, u32[]{:S(2)}) collective-permute-start(bf16[224,128]{1,0:T(8,128)(2,1)S(1)} %add_convert_fusion.1), channel_id=1, source_target_pairs={{0,1},{1,0},{2,3},{3,2},{4,5},{5,4},{6,7},{7,6},{8,9},{9,8},{10,11... | collective-permute-start | bytes 172040 | tf_op jit(solution)/shard_map/ppermute | solution.py:331
  20.2 5.8 %collective-permute-start.5 = (bf16[224,128]{1,0:T(8,128)(2,1)S(1)}, bf16[224,128]{1,0:T(8,128)(2,1)S(1)}, u32[]{:S(2)}, u32[]{:S(2)}) collective-permute-start(bf16[224,128]{1,0:T(8,128)(2,1)S(1)} %add_convert_fusion.1), channel_id=1, source_target_pairs={{0,2},{1,3},{2,0},{3,1},{4,6},{5,7},{6,4},{7,5},{8,10},{9,11},{10,... | collective-permute-start | bytes 172040 | tf_op jit(solution)/shard_map/ppermute | solution.py:331
  21.4 6.0 %collective-permute-start.6 = (bf16[224,128]{1,0:T(8,128)(2,1)S(1)}, bf16[224,128]{1,0:T(8,128)(2,1)S(1)}, u32[]{:S(2)}, u32[]{:S(2)}) collective-permute-start(bf16[224,128]{1,0:T(8,128)(2,1)S(1)} %add_convert_fusion.1), channel_id=1, source_target_pairs={{0,3},{1,2},{2,1},{3,0},{4,7},{5,6},{6,5},{7,4},{8,11},{9,10},{10,... | collective-permute-start | bytes 172040 | tf_op jit(solution)/shard_map/ppermute | solution.py:331
  27.4 4.2 %collective-permute-start.7 = (bf16[224,128]{1,0:T(8,128)(2,1)S(1)}, bf16[224,128]{1,0:T(8,128)(2,1)S(1)}, u32[]{:S(2)}, u32[]{:S(2)}) collective-permute-start(bf16[224,128]{1,0:T(8,128)(2,1)S(1)} %add_convert_fusion.near0), channel_id=1, source_target_pairs={{0,8},{1,9},{2,10},{3,11},{4,12},{5,13},{6,14},{7,15},{8,0},{9,1},... | collective-permute-start | bytes 172040 | tf_op jit(solution)/shard_map/ppermute | solution.py:331
  29.4 4.2 %collective-permute-start.8 = (bf16[224,128]{1,0:T(8,128)(2,1)S(1)}, bf16[224,128]{1,0:T(8,128)(2,1)S(1)}, u32[]{:S(2)}, u32[]{:S(2)}) collective-permute-start(bf16[224,128]{1,0:T(8,128)(2,1)S(1)} %add_convert_fusion.near0), channel_id=1, source_target_pairs={{0,16},{1,17},{2,18},{3,19},{4,20},{5,21},{6,22},{7,23},{8,24},{9,... | collective-permute-start | bytes 172040 | tf_op jit(solution)/shard_map/ppermute | solution.py:331
  29.5 5.1 %collective-permute-start.9 = (bf16[224,128]{1,0:T(8,128)(2,1)S(1)}, bf16[224,128]{1,0:T(8,128)(2,1)S(1)}, u32[]{:S(2)}, u32[]{:S(2)}) collective-permute-start(bf16[224,128]{1,0:T(8,128)(2,1)S(1)} %add_convert_fusion.near0), channel_id=1, source_target_pairs={{0,24},{1,25},{2,26},{3,27},{4,28},{5,29},{6,30},{7,31},{8,16},{9,... | collective-permute-start | bytes 172040 | tf_op jit(solution)/shard_map/ppermute | solution.py:331
  34.6 0.7 %copy-start.2 = (f32[768]{0:T(1024)S(1)}, f32[768]{0:T(1024)}, u32[]{:S(2)}) copy-start(f32[768]{0:T(1024)} %gain_ref.1) | copy-start | bytes 9220
  34.7 2.3 %collective-permute-start.10 = (bf16[896,128]{1,0:T(8,128)(2,1)S(1)}, bf16[896,128]{1,0:T(8,128)(2,1)S(1)}, u32[]{:S(2)}, u32[]{:S(2)}) collective-permute-start(bf16[896,128]{1,0:T(8,128)(2,1)S(1)} %pad_maximum_fusion), channel_id=1, source_target_pairs={{0,4},{1,5},{2,6},{3,7},{4,0},{5,1},{6,2},{7,3},{8,12},{9,13},{10,... | collective-permute-start | bytes 688136 | tf_op jit(solution)/shard_map/ppermute | solution.py:331

commit v4 on v3

--- a/solution.py
+++ b/solution.py
@@ -151,15 +151,17 @@
     w_out_s[...] = jnp.transpose(w_out_ref[...])
     bias_s[...] = as_column(b_in_ref[...].reshape(1, hidden))
 
-    chunk = 256
+    chunk = width
     third = places // 3
 
     def image(first, count, window):
         first = pl.multiple_of(first, TILE)
         limit = count * TILE
-        lane = lax.broadcasted_iota(jnp.int32, (hidden, window), 1)
-        own_in = jnp.where(lane < limit, w_in_t[:, :window].astype(f32), 0.0).astype(bf16)
-        own_out = jnp.where(lane < limit, w_out_s[:, :window].astype(f32), 0.0).astype(bf16)
+        lane = lax.broadcasted_iota(jnp.int32, (16, window), 1)
+        own_lane = jnp.where(lane < limit, 1.0, 0.0).astype(bf16)
+        own_lane = jnp.concatenate([own_lane] * (hidden // 16), axis=0)
+        own_in = w_in_t[:, :window] * own_lane
+        own_out = w_out_s[:, :window] * own_lane
         bias = jnp.concatenate([bias_s[...]] * (chunk // LANES), axis=1)
         gin = jnp.zeros((window, hidden), f32)
         gout = jnp.zeros((window, hidden), f32)

time: 38.2 us -> 38.3 us (level)
  no operation moved by 1% of the time
where the time goes in v4:
time: 38.3 us; the launch traced here: 38.1 us
  starting transfers between devices  16.3 us (43%)
  waiting for transfers between devices  14.5 us (38%)
  Pallas kernels  5.82 us (15%)
  between operations  0.72 us (2%)
  local copies, waits for them, and re-layouts  0.63 us (2%)
    ppermute x11, starting transfers between devices, swap(): return lax.ppermute(x, AXES, [(i, i ^ mask) for i in range(devices)])  16.3 us
    ppermute x11, waiting for transfers between devices, swap(): return lax.ppermute(x, AXES, [(i, i ^ mask) for i in range(devices)])  14.5 us
    pallas_call x1, Pallas kernels, all_terms(): pl.pallas_call(functools.partial(grad_kernel, pair), name='terms', out_sh...  3.12 us
    pallas_call x1, Pallas kernels, all_terms(): pl.pallas_call(token_kernel, name='rows', out_shape=jax.ShapeDtypeStruct(...  1.6 us
    pallas_call x1, Pallas kernels, clipped(): pl.pallas_call(functools.partial(clip_kernel, pair), name='clip', out_sha...  1.11 us
  transfers between devices with their start and end apart: 11, of which 10 were waited for; matrix products, arithmetic and copies ran while one was open for 0% of the time, Pallas kernels for 4%

profile of v4, /device:TPU:0, one launch (start us, length us, event | category | flops | bytes accessed | tf_op | source)
XLA Modules:
  0.0 38.1 jit_solution(9316000203770695065)
XLA Ops:
  0.6 3.1 %terms.1 = (f32[896,128]{1,0:T(8,128)S(1)}, bf16[896,128]{1,0:T(8,128)(2,1)S(1)}, bf16[608,768]{1,0:T(8,128)(2,1)S(1)}, f32[320,128]{1,0:T(8,128)S(1)}, f32[320,128]{1,0:T(8,128)S(1)}, /*index=5*/f32[320,128]{1,0:T(8,128)S(1)}) custom-call(s32[1]{0:T(128)} %bitcast.me_ref, s32[3,32]{1,0:T(4,128)} %bitcast.6, s32[3,32]{1,0:T(4,128)} %bitcast.7, ...), custom_call_target="tpu_custom_call" | custom-call | tf_op jit(solution)/shard_map/terms/pallas_call | solution.py:266
  3.8 2.9 %collective-permute-start = (bf16[896,128]{1,0:T(8,128)(2,1)S(1)}, bf16[896,128]{1,0:T(8,128)(2,1)S(1)}, u32[]{:S(2)}, u32[]{:S(2)}) collective-permute-start(bf16[896,128]{1,0:T(8,128)(2,1)S(1)} %get-tuple-element.24), channel_id=1, source_target_pairs={{0,4},{1,5},{2,6},{3,7},{4,0},{5,1},{6,2},{7,3},{8,12},{9,13},{10,... | collective-permute-start | bytes 688136 | tf_op jit(solution)/shard_map/ppermute | solution.py:333
  6.7 1.1 %collective-permute-done = bf16[896,128]{1,0:T(8,128)(2,1)S(1)} collective-permute-done((bf16[896,128]{1,0:T(8,128)(2,1)S(1)}, bf16[896,128]{1,0:T(8,128)(2,1)S(1)}, u32[]{:S(2)}, u32[]{:S(2)}) %collective-permute-start) | collective-permute-done | bytes 229408 | tf_op jit(solution)/shard_map/ppermute | solution.py:333
  7.9 2.9 %collective-permute-start.1 = (bf16[224,128]{1,0:T(8,128)(2,1)S(1)}, bf16[224,128]{1,0:T(8,128)(2,1)S(1)}, u32[]{:S(2)}, u32[]{:S(2)}) collective-permute-start(bf16[224,128]{1,0:T(8,128)(2,1)S(1)} %get-tuple-element.31), channel_id=1, source_target_pairs={{0,8},{1,9},{2,10},{3,11},{4,12},{5,13},{6,14},{7,15},{8,0},{9,1},... | collective-permute-start | bytes 172040 | tf_op jit(solution)/shard_map/ppermute | solution.py:333
  10.8 1.5 %collective-permute-start.2 = (bf16[224,128]{1,0:T(8,128)(2,1)S(1)}, bf16[224,128]{1,0:T(8,128)(2,1)S(1)}, u32[]{:S(2)}, u32[]{:S(2)}) collective-permute-start(bf16[224,128]{1,0:T(8,128)(2,1)S(1)} %get-tuple-element.33), channel_id=1, source_target_pairs={{0,16},{1,17},{2,18},{3,19},{4,20},{5,21},{6,22},{7,23},{8,24},{9,... | collective-permute-start | bytes 172040 | tf_op jit(solution)/shard_map/ppermute | solution.py:333
  12.4 0.0 collective-permute-start.3
  12.4 0.0 copy-start
  12.4 0.0 copy-start.1
  12.4 0.7 %collective-permute-done.1 = bf16[224,128]{1,0:T(8,128)(2,1)S(1)} collective-permute-done((bf16[224,128]{1,0:T(8,128)(2,1)S(1)}, bf16[224,128]{1,0:T(8,128)(2,1)S(1)}, u32[]{:S(2)}, u32[]{:S(2)}) %collective-permute-start.1) | collective-permute-done | bytes 57376 | tf_op jit(solution)/shard_map/ppermute | solution.py:333
  13.1 2.0 %collective-permute-done.2 = bf16[224,128]{1,0:T(8,128)(2,1)S(1)} collective-permute-done((bf16[224,128]{1,0:T(8,128)(2,1)S(1)}, bf16[224,128]{1,0:T(8,128)(2,1)S(1)}, u32[]{:S(2)}, u32[]{:S(2)}) %collective-permute-start.2) | collective-permute-done | bytes 57376 | tf_op jit(solution)/shard_map/ppermute | solution.py:333
  15.0 2.4 %collective-permute-done.3 = bf16[224,128]{1,0:T(8,128)(2,1)S(1)} collective-permute-done((bf16[224,128]{1,0:T(8,128)(2,1)S(1)}, bf16[224,128]{1,0:T(8,128)(2,1)S(1)}, u32[]{:S(2)}, u32[]{:S(2)}) %collective-permute-start.3) | collective-permute-done | bytes 57376 | tf_op jit(solution)/shard_map/ppermute | solution.py:333
  17.5 2.8 %collective-permute-start.4 = (bf16[224,128]{1,0:T(8,128)(2,1)S(1)}, bf16[224,128]{1,0:T(8,128)(2,1)S(1)}, u32[]{:S(2)}, u32[]{:S(2)}) collective-permute-start(bf16[224,128]{1,0:T(8,128)(2,1)S(1)} %add_convert_fusion.1), channel_id=1, source_target_pairs={{0,1},{1,0},{2,3},{3,2},{4,5},{5,4},{6,7},{7,6},{8,9},{9,8},{10,11... | collective-permute-start | bytes 172040 | tf_op jit(solution)/shard_map/ppermute | solution.py:333
  20.3 1.2 %collective-permute-start.5 = (bf16[224,128]{1,0:T(8,128)(2,1)S(1)}, bf16[224,128]{1,0:T(8,128)(2,1)S(1)}, u32[]{:S(2)}, u32[]{:S(2)}) collective-permute-start(bf16[224,128]{1,0:T(8,128)(2,1)S(1)} %add_convert_fusion.1), channel_id=1, source_target_pairs={{0,2},{1,3},{2,0},{3,1},{4,6},{5,7},{6,4},{7,5},{8,10},{9,11},{10,... | collective-permute-start | bytes 172040 | tf_op jit(solution)/shard_map/ppermute | solution.py:333
  21.5 1.3 %collective-permute-start.6 = (bf16[224,128]{1,0:T(8,128)(2,1)S(1)}, bf16[224,128]{1,0:T(8,128)(2,1)S(1)}, u32[]{:S(2)}, u32[]{:S(2)}) collective-permute-start(bf16[224,128]{1,0:T(8,128)(2,1)S(1)} %add_convert_fusion.1), channel_id=1, source_target_pairs={{0,3},{1,2},{2,1},{3,0},{4,7},{5,6},{6,5},{7,4},{8,11},{9,10},{10,... | collective-permute-start | bytes 172040 | tf_op jit(solution)/shard_map/ppermute | solution.py:333
  22.7 0.3 collective-permute-done.4
  23.1 3.0 %collective-permute-done.5 = bf16[224,128]{1,0:T(8,128)(2,1)S(1)} collective-permute-done((bf16[224,128]{1,0:T(8,128)(2,1)S(1)}, bf16[224,128]{1,0:T(8,128)(2,1)S(1)}, u32[]{:S(2)}, u32[]{:S(2)}) %collective-permute-start.5) | collective-permute-done | bytes 57376 | tf_op jit(solution)/shard_map/ppermute | solution.py:333
  26.1 1.3 %collective-permute-done.6 = bf16[224,128]{1,0:T(8,128)(2,1)S(1)} collective-permute-done((bf16[224,128]{1,0:T(8,128)(2,1)S(1)}, bf16[224,128]{1,0:T(8,128)(2,1)S(1)}, u32[]{:S(2)}, u32[]{:S(2)}) %collective-permute-start.6) | collective-permute-done | bytes 57376 | tf_op jit(solution)/shard_map/ppermute | solution.py:333
  27.5 2.0 %collective-permute-start.7 = (bf16[224,128]{1,0:T(8,128)(2,1)S(1)}, bf16[224,128]{1,0:T(8,128)(2,1)S(1)}, u32[]{:S(2)}, u32[]{:S(2)}) collective-permute-start(bf16[224,128]{1,0:T(8,128)(2,1)S(1)} %add_convert_fusion.near0), channel_id=1, source_target_pairs={{0,8},{1,9},{2,10},{3,11},{4,12},{5,13},{6,14},{7,15},{8,0},{9,1},... | collective-permute-start | bytes 172040 | tf_op jit(solution)/shard_map/ppermute | solution.py:333
  29.5 0.1 collective-permute-start.8
  29.6 1.4 %collective-permute-start.9 = (bf16[224,128]{1,0:T(8,128)(2,1)S(1)}, bf16[224,128]{1,0:T(8,128)(2,1)S(1)}, u32[]{:S(2)}, u32[]{:S(2)}) collective-permute-start(bf16[224,128]{1,0:T(8,128)(2,1)S(1)} %add_convert_fusion.near0), channel_id=1, source_target_pairs={{0,24},{1,25},{2,26},{3,27},{4,28},{5,29},{6,30},{7,31},{8,16},{9,... | collective-permute-start | bytes 172040 | tf_op jit(solution)/shard_map/ppermute | solution.py:333
  31.0 0.7 %collective-permute-done.7.near1 = bf16[224,128]{1,0:T(8,128)(2,1)S(1)} collective-permute-done((bf16[224,128]{1,0:T(8,128)(2,1)S(1)}, bf16[224,128]{1,0:T(8,128)(2,1)S(1)}, u32[]{:S(2)}, u32[]{:S(2)}) %collective-permute-start.7) | collective-permute-done | bytes 57376 | tf_op jit(solution)/shard_map/ppermute | solution.py:333
  31.7 1.9 %collective-permute-done.8.near2 = bf16[224,128]{1,0:T(8,128)(2,1)S(1)} collective-permute-done((bf16[224,128]{1,0:T(8,128)(2,1)S(1)}, bf16[224,128]{1,0:T(8,128)(2,1)S(1)}, u32[]{:S(2)}, u32[]{:S(2)}) %collective-permute-start.8) | collective-permute-done | bytes 57376 | tf_op jit(solution)/shard_map/ppermute | solution.py:333
  33.7 1.0 %collective-permute-done.9.near3 = bf16[224,128]{1,0:T(8,128)(2,1)S(1)} collective-permute-done((bf16[224,128]{1,0:T(8,128)(2,1)S(1)}, bf16[224,128]{1,0:T(8,128)(2,1)S(1)}, u32[]{:S(2)}, u32[]{:S(2)}) %collective-permute-start.9) | collective-permute-done | bytes 57376 | tf_op jit(solution)/shard_map/ppermute | solution.py:333
  34.7 0.0 copy-start.2
  34.7 0.1 collective-permute-start.10
  34.8 0.0 copy-done
  34.8 0.0 copy-done.1
  34.8 0.6 %copy-done.2 = f32[768]{0:T(1024)S(1)} copy-done((f32[768]{0:T(1024)S(1)}, f32[768]{0:T(1024)}, u32[]{:S(2)}) %copy-start.2) | copy-done | bytes 3096
  35.4 1.6 %rows.1 = bf16[320,768]{1,0:T(8,128)(2,1)} custom-call(bf16[320,768]{1,0:T(8,128)(2,1)S(1)} %copy-done, bf16[320,768]{1,0:T(8,128)(2,1)S(1)} %copy-done.1, f32[768]{0:T(1024)S(1)} %copy-done.2, bf16[608,768]{1,0:T(8,128)(2,1)S(1)} %get-tuple-element.19.dn_ref, f32[320,128]{1,0:T(8,128)S(1)} %get-tuple-element.20.alive_s, ...), custom_call_target="tpu_custom_call" | custom-call | tf_op jit(solution)/shard_map/rows/pallas_call | solution.py:321
  37.0 0.0 collective-permute-done.10.far_ref
  37.0 1.1 %clip.1 = (bf16[288,384]{1,0:T(8,128)(2,1)}, bf16[384]{0:T(512)(128)(2,1)}, bf16[288,384]{1,0:T(8,128)(2,1)}, bf16[288]{0:T(512)(128)(2,1)}, bf16[768]{0:T(1024)(128)(2,1)}, /*index=5*/bf16[768]{0:T(1024)(128)(2,1)}) custom-call(s32[1]{0:T(128)} %bitcast.me_ref, bf16[224,128]{1,0:T(8,128)(2,1)S(1)} %add_convert_fusion.near0, ...), custom_call_target="tpu_custom_call" | custom-call | tf_op jit(solution)/shard_map/clip/pallas_call | solution.py:428
  (5 shorter events, 0.2 us)
Async XLA Ops:
  3.8 4.1 %collective-permute-start = (bf16[896,128]{1,0:T(8,128)(2,1)S(1)}, bf16[896,128]{1,0:T(8,128)(2,1)S(1)}, u32[]{:S(2)}, u32[]{:S(2)}) collective-permute-start(bf16[896,128]{1,0:T(8,128)(2,1)S(1)} %get-tuple-element.24), channel_id=1, source_target_pairs={{0,4},{1,5},{2,6},{3,7},{4,0},{5,1},{6,2},{7,3},{8,12},{9,13},{10,... | collective-permute-start | bytes 688136 | tf_op jit(solution)/shard_map/ppermute | solution.py:333
  7.9 5.1 %collective-permute-start.1 = (bf16[224,128]{1,0:T(8,128)(2,1)S(1)}, bf16[224,128]{1,0:T(8,128)(2,1)S(1)}, u32[]{:S(2)}, u32[]{:S(2)}) collective-permute-start(bf16[224,128]{1,0:T(8,128)(2,1)S(1)} %get-tuple-element.31), channel_id=1, source_target_pairs={{0,8},{1,9},{2,10},{3,11},{4,12},{5,13},{6,14},{7,15},{8,0},{9,1},... | collective-permute-start | bytes 172040 | tf_op jit(solution)/shard_map/ppermute | solution.py:333
  10.8 4.2 %collective-permute-start.2 = (bf16[224,128]{1,0:T(8,128)(2,1)S(1)}, bf16[224,128]{1,0:T(8,128)(2,1)S(1)}, u32[]{:S(2)}, u32[]{:S(2)}) collective-permute-start(bf16[224,128]{1,0:T(8,128)(2,1)S(1)} %get-tuple-element.33), channel_id=1, source_target_pairs={{0,16},{1,17},{2,18},{3,19},{4,20},{5,21},{6,22},{7,23},{8,24},{9,... | collective-permute-start | bytes 172040 | tf_op jit(solution)/shard_map/ppermute | solution.py:333
  12.4 5.1 %collective-permute-start.3 = (bf16[224,128]{1,0:T(8,128)(2,1)S(1)}, bf16[224,128]{1,0:T(8,128)(2,1)S(1)}, u32[]{:S(2)}, u32[]{:S(2)}) collective-permute-start(bf16[224,128]{1,0:T(8,128)(2,1)S(1)} %get-tuple-element.32), channel_id=1, source_target_pairs={{0,24},{1,25},{2,26},{3,27},{4,28},{5,29},{6,30},{7,31},{8,16},{9,... | collective-permute-start | bytes 172040 | tf_op jit(solution)/shard_map/ppermute | solution.py:333
  12.4 22.4 %copy-start = (bf16[320,768]{1,0:T(8,128)(2,1)S(1)}, bf16[320,768]{1,0:T(8,128)(2,1)}, u32[]{:S(2)}) copy-start(bf16[320,768]{1,0:T(8,128)(2,1)} %tok_ref.1) | copy-start | bytes 1474564
  12.4 22.5 %copy-start.1 = (bf16[320,768]{1,0:T(8,128)(2,1)S(1)}, bf16[320,768]{1,0:T(8,128)(2,1)}, u32[]{:S(2)}) copy-start(bf16[320,768]{1,0:T(8,128)(2,1)} %cot_ref.1) | copy-start | bytes 1474564
  17.5 5.6 %collective-permute-start.4 = (bf16[224,128]{1,0:T(8,128)(2,1)S(1)}, bf16[224,128]{1,0:T(8,128)(2,1)S(1)}, u32[]{:S(2)}, u32[]{:S(2)}) collective-permute-start(bf16[224,128]{1,0:T(8,128)(2,1)S(1)} %add_convert_fusion.1), channel_id=1, source_target_pairs={{0,1},{1,0},{2,3},{3,2},{4,5},{5,4},{6,7},{7,6},{8,9},{9,8},{10,11... | collective-permute-start | bytes 172040 | tf_op jit(solution)/shard_map/ppermute | solution.py:333
  20.3 5.8 %collective-permute-start.5 = (bf16[224,128]{1,0:T(8,128)(2,1)S(1)}, bf16[224,128]{1,0:T(8,128)(2,1)S(1)}, u32[]{:S(2)}, u32[]{:S(2)}) collective-permute-start(bf16[224,128]{1,0:T(8,128)(2,1)S(1)} %add_convert_fusion.1), channel_id=1, source_target_pairs={{0,2},{1,3},{2,0},{3,1},{4,6},{5,7},{6,4},{7,5},{8,10},{9,11},{10,... | collective-permute-start | bytes 172040 | tf_op jit(solution)/shard_map/ppermute | solution.py:333
  21.5 6.0 %collective-permute-start.6 = (bf16[224,128]{1,0:T(8,128)(2,1)S(1)}, bf16[224,128]{1,0:T(8,128)(2,1)S(1)}, u32[]{:S(2)}, u32[]{:S(2)}) collective-permute-start(bf16[224,128]{1,0:T(8,128)(2,1)S(1)} %add_convert_fusion.1), channel_id=1, source_target_pairs={{0,3},{1,2},{2,1},{3,0},{4,7},{5,6},{6,5},{7,4},{8,11},{9,10},{10,... | collective-permute-start | bytes 172040 | tf_op jit(solution)/shard_map/ppermute | solution.py:333
  27.5 4.2 %collective-permute-start.7 = (bf16[224,128]{1,0:T(8,128)(2,1)S(1)}, bf16[224,128]{1,0:T(8,128)(2,1)S(1)}, u32[]{:S(2)}, u32[]{:S(2)}) collective-permute-start(bf16[224,128]{1,0:T(8,128)(2,1)S(1)} %add_convert_fusion.near0), channel_id=1, source_target_pairs={{0,8},{1,9},{2,10},{3,11},{4,12},{5,13},{6,14},{7,15},{8,0},{9,1},... | collective-permute-start | bytes 172040 | tf_op jit(solution)/shard_map/ppermute | solution.py:333
  29.5 4.2 %collective-permute-start.8 = (bf16[224,128]{1,0:T(8,128)(2,1)S(1)}, bf16[224,128]{1,0:T(8,128)(2,1)S(1)}, u32[]{:S(2)}, u32[]{:S(2)}) collective-permute-start(bf16[224,128]{1,0:T(8,128)(2,1)S(1)} %add_convert_fusion.near0), channel_id=1, source_target_pairs={{0,16},{1,17},{2,18},{3,19},{4,20},{5,21},{6,22},{7,23},{8,24},{9,... | collective-permute-start | bytes 172040 | tf_op jit(solution)/shard_map/ppermute | solution.py:333
  29.6 5.1 %collective-permute-start.9 = (bf16[224,128]{1,0:T(8,128)(2,1)S(1)}, bf16[224,128]{1,0:T(8,128)(2,1)S(1)}, u32[]{:S(2)}, u32[]{:S(2)}) collective-permute-start(bf16[224,128]{1,0:T(8,128)(2,1)S(1)} %add_convert_fusion.near0), channel_id=1, source_target_pairs={{0,24},{1,25},{2,26},{3,27},{4,28},{5,29},{6,30},{7,31},{8,16},{9,... | collective-permute-start | bytes 172040 | tf_op jit(solution)/shard_map/ppermute | solution.py:333
  34.7 0.7 %copy-start.2 = (f32[768]{0:T(1024)S(1)}, f32[768]{0:T(1024)}, u32[]{:S(2)}) copy-start(f32[768]{0:T(1024)} %gain_ref.1) | copy-start | bytes 9220
  34.7 2.3 %collective-permute-start.10 = (bf16[896,128]{1,0:T(8,128)(2,1)S(1)}, bf16[896,128]{1,0:T(8,128)(2,1)S(1)}, u32[]{:S(2)}, u32[]{:S(2)}) collective-permute-start(bf16[896,128]{1,0:T(8,128)(2,1)S(1)} %pad_maximum_fusion), channel_id=1, source_target_pairs={{0,4},{1,5},{2,6},{3,7},{4,0},{5,1},{6,2},{7,3},{8,12},{9,13},{10,... | collective-permute-start | bytes 688136 | tf_op jit(solution)/shard_map/ppermute | solution.py:333
